TPU v7x, 256 devices: a whole 4x4x8 slice. The times are simulated.
256 devices in a mesh: dp: 16 (over z_lo, x), shard: 16 (over z_hi, y, core).
Axes of the slice: x: 4, y: 4, z: 8 (z_hi: 2, z_lo: 4; z = z_hi * 4 + z_lo), core: 2. Of those that a mesh axis runs over, the one named last changes fastest.
Arguments:
- hidden_in: bfloat16 [65536, 5120], P(('dp', 'shard')), may hold values from -24 to 24
- teacher: bfloat16 [65536, 768], P(('dp', 'shard')), may hold values from -6 to 6
- norm_gain: bfloat16 [5120], P('shard'), may hold values from 0.5 to 1.5
- w_key: bfloat16 [5120, 768], P('shard'), may hold values from -0.078125 to 0.078125
- group_rows: int32 [16], P('dp'), may hold values from 64 to 256
- member: int32 [16, 16], P('dp', 'shard'), may hold values from 0 to 1, as said below
Outputs:
- loss: float32 [], replicated
- grad_gain: float32 [5120], P('shard')
- grad_key: float32 [5120, 768], P('shard')
Inputs may be any that keep to these rules, and one draw needn't show every extreme that they name: The first group_rows[p] token slots of each surviving device of group p hold valid tokens. `member`: 1 marks a surviving device; the first device of every group survives.
All inputs are finite; a program needn't handle non-finite values.
Results may differ from a plain program's by a relative error of at most 0.0023.
Values may be sent and summed in bfloat16 or wider, within the bound.
A program may use at most 128 MiB of HBM per device.

v0:
```python
import functools

import jax
import jax.numpy as jnp
from jax import lax
from jax.sharding import Mesh
from jax.sharding import PartitionSpec as P

SHARD = ("shard_0", "shard_1", "shard_2")
DP_SHARD = ("dp_0", "dp_1", "shard_0", "shard_1", "shard_2")
DP = ("dp_0", "dp_1")


EPSILON = 1e-06
SCALE = 1024.0


def in_one_piece(arrays, axis, dim, along):
    columns = [a.reshape(*a.shape[:along], -1) for a in arrays]
    both = jnp.concatenate(columns, axis=along)
    whole, at, finished = (lax.all_gather(both, axis, axis=dim, tiled=True), 0, [])
    for a, column in zip(arrays, columns):
        piece = whole[..., at : at + column.shape[along]]
        finished.append(piece.reshape(*piece.shape[:along], *a.shape[along:]))
        at += column.shape[along]
    return tuple(finished)


def over_axes(value, axes):
    return functools.reduce(lax.psum, axes, value)


def cut_along(value, dim, count):
    before, after = (value.shape[:dim], value.shape[dim + 1 :])
    return jnp.moveaxis(value.reshape(*before, count, -1, *after), dim, 0)


def summed_on_arrival(value, axis, dim):
    blocks = cut_along(value, dim, lax.axis_size(axis))
    arrived = lax.all_to_all(blocks, axis, split_axis=0, concat_axis=0, tiled=True)
    return arrived.sum(axis=0)


def rows_for(lines, count):
    spare = -lines.shape[0] % count
    if not spare:
        return lines
    return jnp.concatenate([lines, jnp.zeros((spare, *lines.shape[1:]), lines.dtype)])


def laid_out(blocks, dim):
    lengths = list(blocks.shape[1:])
    lengths[dim] *= blocks.shape[0]
    return jnp.moveaxis(blocks, 0, dim).reshape(lengths)


def from_everyone(value, axis):
    copies = jnp.broadcast_to(value, (lax.axis_size(axis), *value.shape))
    return lax.all_to_all(copies, axis, split_axis=0, concat_axis=0, tiled=True)


def gather_directly(value, axis, dim):
    return laid_out(from_everyone(value, axis), dim)


def total_of(value, axes):
    padded = rows_for(value, lax.axis_size(axes))
    whole = gather_directly(summed_on_arrival(padded, axes, 0), axes, 0)
    return lax.slice_in_dim(whole, 0, len(value)).reshape(value.shape)


def in_one(arrays, axis):
    ends = [0]
    for a in arrays:
        ends.append(ends[-1] + a.size)
    so_far = total_of(jnp.concatenate([a.ravel() for a in arrays]), axis)
    return tuple((so_far[b:e].reshape(a.shape) for a, b, e in zip(arrays, ends, ends[1:])))


def contract_rows(left, right):
    return lax.dot_general(
        left, right, (((0,), (0,)), ((), ())), preferred_element_type=jnp.float32
    )


def contract_cols(left, right):
    return lax.dot_general(
        left, right, (((1,), (1,)), ((), ())), preferred_element_type=jnp.float32
    )


def fold_terms(columns, piece):
    return contract_rows(columns, piece)


def body(hidden_in, teacher, norm_gain, w_key, group_rows, member):
    rows, width = hidden_in.shape
    features = w_key.shape[1]
    live_rows = group_rows[0]
    alive = member[0, 0]
    position = lax.broadcasted_iota(jnp.int32, (rows, 1), 0)
    valid = jnp.where((position < live_rows) & (alive == 1), 1.0, 0.0).astype(jnp.float32)
    own_count = (alive * live_rows).astype(jnp.float32)
    values = hidden_in.astype(jnp.float32)
    inverse_rms = lax.rsqrt(jnp.mean(values * values, axis=1, keepdims=True) + EPSILON)
    scaled = values * inverse_rms
    gains, key_full = in_one_piece((norm_gain, w_key), SHARD, 0, 1)
    normed = (scaled * gains.astype(jnp.float32)).astype(jnp.bfloat16)
    keys = jnp.dot(normed, key_full, preferred_element_type=jnp.float32)
    diff = keys - teacher.astype(jnp.float32)
    own_sum = jnp.sum(valid * diff * diff)
    total_sum, total_count = (over_axes(own_sum, DP_SHARD), over_axes(own_count, DP_SHARD))
    loss = total_sum / (2.0 * features * total_count)
    upstream = (SCALE / total_count * valid * diff).astype(jnp.bfloat16)
    dnormed = contract_cols(upstream, key_full)
    term_gain = jnp.sum(dnormed * scaled, axis=0)
    columns = lax.all_to_all(normed, SHARD, split_axis=1, concat_axis=0, tiled=True)
    key_piece = fold_terms(columns, lax.all_gather(upstream, SHARD, axis=0, tiled=True))
    gain_piece = summed_on_arrival(term_gain, SHARD, 0)
    grad_gain, grad_key = in_one((gain_piece, key_piece), DP)
    return (loss, grad_gain, grad_key)


def solution(mesh):
    split = Mesh(
        mesh.devices.reshape(4, 4, 2, 4, 2), ("dp_0", "dp_1", "shard_0", "shard_1", "shard_2")
    )
    return jax.shard_map(
        body,
        mesh=split,
        in_specs=(
            P(DP_SHARD, None),
            P(DP_SHARD, None),
            P(SHARD),
            P(SHARD, None),
            P(DP),
            P(DP, SHARD),
        ),
        out_specs=(P(), P(SHARD), P(SHARD, None)),
        check_vma=False,
    )
```

profile of v0, /device:TPU:1, one launch (start us, length us, event | category | flops | bytes accessed | tf_op | source)
XLA Modules:
  0.0 393.0 jit_solution(10601007652579247943)
XLA Ops:
  7.2 0.0 copy-start
  7.2 0.0 all-gather.3.cloned.1.call-start
  7.2 0.9 reshape.67
  8.2 2.1 pad_maximum_fusion.1
  10.3 0.0 all-gather.3.cloned.1.call-update
  10.3 0.0 all-gather.5.cloned.1.call-start
  11.6 2.3 fusion.9
  14.0 112.8 %all-gather.3.cloned.1.call-done = bf16[5120,769]{1,0:T(8,128)(2,1)} async-done(((bf16[320,769]{1,0:T(8,128)(2,1)}), bf16[5120,769]{1,0:T(8,128)(2,1)}) %all-gather.3.cloned.1.call-update) | async-done | bytes 7874576 | tf_op jit(solution)/shard_map/all_gather | solution.py:21
  126.8 1.7 convert_reduce_fusion
  128.5 0.0 copy-done
  128.5 0.8 fusion.8
  129.3 0.0 copy-start.1
  129.3 8.5 %fusion.16 = (f32[]{:T(128)}, f32[256,768]{1,0:T(8,128)S(1)}) fusion(f32[256]{0:T(256)S(1)} %and_select_fusion, bf16[256,768]{1,0:T(8,128)(2,1)} %param.7, bf16[256,5120]{1,0:T(8,128)(2,1)S(1)} %fusion.8, bf16[5120,769]{1,0:T(8,128)(2,1)} %all-gather.3.cloned.1.call-done), kind=kOutput, calls=%fused_computation.15 | convolution fusion | flops 2014248960 | bytes 11666436 | tf_op jit(solution)/shard_map/dot_general | solution.py:109
  137.8 0.0 copy-done.1
  137.8 10.4 %all-reduce.2 = (f32[]{:T(128)}, f32[]{:T(128)}) all-reduce(f32[]{:T(128)} %get-tuple-element.13, f32[]{:T(128)S(6)} %convert_element_type.30), channel_id=1, replica_groups=mesh['dp_0'=4,'dp_1'=4,'shard_0'=2,'shard_1'=4,'shard_2'=2] {'dp_0'}, use_global_device_ids=true, to_apply=%region_2.3 | all-reduce | flops 2 | bytes 16 | tf_op jit(solution)/shard_map/psum | solution.py:30
  148.2 9.0 %all-reduce.1 = (f32[]{:T(128)}, f32[]{:T(128)}) all-reduce(f32[]{:T(128)} %get-tuple-element.7, f32[]{:T(128)} %get-tuple-element.8), channel_id=1, replica_groups=mesh['dp_0'=4,'dp_1'=4,'shard_0'=2,'shard_1'=4,'shard_2'=2] {'dp_1'}, use_global_device_ids=true, to_apply=%region_3.4 | all-reduce | flops 2 | bytes 16 | tf_op jit(solution)/shard_map/psum | solution.py:30
  157.2 8.3 %all-reduce.4 = (f32[]{:T(128)}, f32[]{:T(128)}) all-reduce(f32[]{:T(128)} %get-tuple-element.5, f32[]{:T(128)} %get-tuple-element.6), channel_id=1, replica_groups=mesh['dp_0'=4,'dp_1'=4,'shard_0'=2,'shard_1'=4,'shard_2'=2] {'shard_0'}, use_global_device_ids=true, to_apply=%region_4.5 | all-reduce | flops 2 | bytes 16 | tf_op jit(solution)/shard_map/psum | solution.py:30
  165.5 7.2 %all-reduce = (f32[]{:T(128)}, f32[]{:T(128)}) all-reduce(f32[]{:T(128)} %get-tuple-element.11, f32[]{:T(128)} %get-tuple-element.12), channel_id=1, replica_groups=mesh['dp_0'=4,'dp_1'=4,'shard_0'=2,'shard_1'=4,'shard_2'=2] {'shard_1'}, use_global_device_ids=true, to_apply=%region_5.6 | all-reduce | flops 2 | bytes 16 | tf_op jit(solution)/shard_map/psum | solution.py:30
  172.7 10.2 %all-reduce.3 = (f32[]{:T(128)}, f32[]{:T(128)}) all-reduce(f32[]{:T(128)} %get-tuple-element.3, f32[]{:T(128)} %get-tuple-element.4), channel_id=1, replica_groups=mesh['dp_0'=4,'dp_1'=4,'shard_0'=2,'shard_1'=4,'shard_2'=2] {'shard_2'}, use_global_device_ids=true, to_apply=%region_6.7 | all-reduce | flops 2 | bytes 16 | tf_op jit(solution)/shard_map/psum | solution.py:30
  183.6 0.9 multiply_convert_fusion
  184.5 0.0 all-gather.5.cloned.1.call-update
  184.5 7.2 %fusion.10 = f32[5120]{0:T(1024)S(1)} fusion(f32[256]{0:T(256)S(1)} %add_rsqrt_fusion, bf16[256,5120]{1,0:T(8,128)(2,1)S(1)} %copy-done, bf16[256,768]{1,0:T(8,128)(2,1)} %multiply_convert_fusion, bf16[5120,769]{1,0:T(8,128)(2,1)} %all-gather.3.cloned.1.call-done), kind=kOutput, calls=%fused_computation.11 | convolution fusion | flops 2018503680 | bytes 10900480 | tf_op jit(solution)/shard_map/dot_general | solution.py:87
  191.7 0.7 all_to_all.30
  192.4 3.6 all-to-all-start
  196.0 4.4 %copy.17 = bf16[256,5120]{0,1:T(8,128)(2,1)} copy(bf16[256,5120]{1,0:T(8,128)(2,1)} %copy-done.1) | data formatting | bytes 5242880 | tf_op jit(solution)/shard_map/convert_element_type | solution.py:108
  200.4 7.5 %all-to-all-done = f32[16,1,320]{2,1,0:T(1,128)S(1)} async-done(((f32[16,1,320]{2,1,0:T(1,128)}), f32[16,1,320]{2,1,0:T(1,128)S(1)}, u32[]{:S(2)}, u32[]{:S(2)}) %all-to-all-start) | async-done | bytes 20512 | tf_op jit(solution)/shard_map/all_to_all | solution.py:40
  207.9 3.9 all-to-all-start.1
  211.9 94.4 %all-to-all-done.1 = bf16[256,16,320]{0,2,1:T(8,128)(2,1)S(1)} async-done(((bf16[256,16,320]{0,2,1:T(8,128)(2,1)}), bf16[256,16,320]{0,2,1:T(8,128)(2,1)S(1)}, u32[]{:S(2)}, u32[]{:S(2)}) %all-to-all-start.1) | async-done | bytes 2621472 | tf_op jit(solution)/shard_map/all_to_all | solution.py:117
  306.3 1.8 copy.22
  308.1 1.8 all-gather.5.cloned.1.call-done
  309.9 5.8 %fusion.17 = f32[320,768]{1,0:T(8,128)S(1)} fusion(bf16[4096,320]{0,1:T(8,128)(2,1)} %bitcast.16, bf16[4096,768]{1,0:T(8,128)(2,1)} %all-gather.5.cloned.1.call-done), kind=kOutput, calls=%fused_computation.21 | convolution fusion | flops 2013265920 | bytes 9895936 | tf_op jit(solution)/shard_map/dot_general | solution.py:81
  315.7 0.1 reshape.63
  315.7 0.3 pad_maximum_fusion
  316.1 1.3 all_to_all.36
  317.4 34.1 %all_to_all.43 = f32[16,1,15380]{2,1,0:T(1,128)S(1)} all-to-all(f32[16,1,15380]{2,1,0:T(1,128)S(1)} %all_to_all.36), channel_id=1, replica_groups=mesh['dp_0'=4,'dp_1'=4,'shard_0'=2,'shard_1'=4,'shard_2'=2] {'dp_0','dp_1'}, dimensions={0} | all-to-all | bytes 1968640 | tf_op jit(solution)/shard_map/all_to_all | solution.py:40
  351.5 0.6 reduce_sum.49
  352.1 1.5 broadcast_in_dim.15
  353.6 5.2 %all-to-all-start.3 = ((f32[16,1,15380]{2,1,0:T(1,128)}), f32[16,1,15380]{2,1,0:T(1,128)S(1)}, u32[]{:S(2)}, u32[]{:S(2)}) async-start(f32[16,1,15380]{2,1,0:T(1,128)} %broadcast_in_dim.15), calls=%async_computation.3 | async-start | bytes 1982464 | tf_op jit(solution)/shard_map/all_to_all | solution.py:59
  360.0 19.9 %all-to-all-done.3 = f32[16,1,15380]{2,1,0:T(1,128)S(1)} async-done(((f32[16,1,15380]{2,1,0:T(1,128)}), f32[16,1,15380]{2,1,0:T(1,128)S(1)}, u32[]{:S(2)}, u32[]{:S(2)}) %all-to-all-start.3) | async-done | bytes 984352 | tf_op jit(solution)/shard_map/all_to_all | solution.py:59
  380.0 2.5 reduce.3
  382.4 0.5 reshape.64
  383.0 0.6 slice.18
  383.5 0.3 slice.19
  383.9 1.1 reshape.65
  (4 shorter events, 0.1 us)
Async XLA Ops:
  7.2 121.3 %copy-start = (bf16[256,5120]{1,0:T(8,128)(2,1)S(1)}, bf16[256,5120]{1,0:T(8,128)(2,1)}, u32[]{:S(2)}) copy-start(bf16[256,5120]{1,0:T(8,128)(2,1)} %param.6) | copy-start | bytes 7864324
  7.2 119.6 %all-gather.3.cloned.1.call-start = ((), (), s32[]{:S(2)}) async-start(), calls=%async_computation.4 | async-start | bytes 9748480 | tf_op jit(solution)/shard_map/all_gather | solution.py:21
  10.3 299.6 %all-gather.5.cloned.1.call-start = ((), (), s32[]{:S(2)}) async-start(), calls=%async_computation.5 | async-start | bytes 6684672 | tf_op jit(solution)/shard_map/all_gather | solution.py:118
  129.3 8.5 %copy-start.1 = (bf16[256,5120]{1,0:T(8,128)(2,1)}, bf16[256,5120]{1,0:T(8,128)(2,1)S(1)}, u32[]{:S(2)}) copy-start(bf16[256,5120]{1,0:T(8,128)(2,1)S(1)} %fusion.8) | copy-start | bytes 7864324
  192.4 15.5 %all-to-all-start = ((f32[16,1,320]{2,1,0:T(1,128)}), f32[16,1,320]{2,1,0:T(1,128)S(1)}, u32[]{:S(2)}, u32[]{:S(2)}) async-start(f32[16,1,320]{2,1,0:T(1,128)} %all_to_all.30), calls=%async_computation | async-start | bytes 49152 | tf_op jit(solution)/shard_map/all_to_all | solution.py:40
  207.9 98.4 %all-to-all-start.1 = ((bf16[256,16,320]{0,2,1:T(8,128)(2,1)}), bf16[256,16,320]{0,2,1:T(8,128)(2,1)S(1)}, u32[]{:S(2)}, u32[]{:S(2)}) async-start(bf16[256,16,320]{0,2,1:T(8,128)(2,1)} %bitcast.2), calls=%async_computation.1 | async-start | bytes 5242880 | tf_op jit(solution)/shard_map/all_to_all | solution.py:117
  353.6 26.4 %all-to-all-start.3 = ((f32[16,1,15380]{2,1,0:T(1,128)}), f32[16,1,15380]{2,1,0:T(1,128)S(1)}, u32[]{:S(2)}, u32[]{:S(2)}) async-start(f32[16,1,15380]{2,1,0:T(1,128)} %broadcast_in_dim.15), calls=%async_computation.3 | async-start | bytes 1982464 | tf_op jit(solution)/shard_map/all_to_all | solution.py:59
Sparse Core Ops, SparseCore 0:
  11.3 115.4 all-gather.2
  184.6 125.2 all-gather.4
where the time goes:
time: 396 us; the launch traced here: 393 us
  waiting for transfers between devices  236 us (60%)
  blocking collectives  79.2 us (20%)
  matrix products  21.5 us (5%)
  between operations  18.5 us (5%)
  local copies, waits for them, and re-layouts  13.3 us (3%)
  starting transfers between devices  12.8 us (3%)
  other arithmetic  11.3 us (3%)
    all_gather x1, waiting for transfers between devices, in_one_piece(): lax.all_gather(both, axis, axis=dim, tiled=True)  113 us
    all_to_all x1, waiting for transfers between devices, body(): lax.all_to_all(normed, SHARD, split_axis=1, concat_axis=0, tiled=True)  94.4 us
    psum x5, blocking collectives, over_axes(): return functools.reduce(lax.psum, axes, value)  45.1 us
    all_to_all x1, blocking collectives, summed_on_arrival(): lax.all_to_all(blocks, axis, split_axis=0, concat_axis=0, tiled=True)  34.1 us
    all_to_all x1, waiting for transfers between devices, from_everyone(): return lax.all_to_all(copies, axis, split_axis=0, concat_axis=0, tiled=True)  19.9 us
    dot_general x1, matrix products, body(): keys = jnp.dot(normed, key_full, preferred_element_type=jnp.float32)  8.52 us
  transfers between devices with their start and end apart: 5, of which 5 were waited for; matrix products, arithmetic and copies ran while one was open for 4% of the time, Pallas kernels for 0%

commit v1 on v0

v1 whole, which is shorter than its diff:
```python
import jax
import jax.numpy as jnp
from jax import lax
from jax.experimental import pallas as pl
from jax.experimental.pallas import tpu as pltpu
from jax.sharding import Mesh
from jax.sharding import PartitionSpec as P

SHARD = ("shard_0", "shard_1", "shard_2")
DP_SHARD = ("dp_0", "dp_1", "shard_0", "shard_1", "shard_2")
DP = ("dp_0", "dp_1")
MESH = pl.DeviceIdType.MESH
F32, BF16 = jnp.float32, jnp.bfloat16

EPSILON = 1e-06
SCALE = 1024.0

TOK = 256
D = 5120
KV = 768
HK = KV // 2
SL = 320
PC = 2 * SL
YB = 2 * PC
QK = HK // 2
XK = QK // 4

SMALL = ("info", "w", "tea", "hid", "lsib", "out")


def slots(*groups):
    place, at = {}, 0
    for name, count in groups:
        place[name] = at
        at += count
    return place, at


SLOT, N_SLOT = slots(
    *((name, 1) for name in SMALL),
    ("ginfo", 8), ("lsh", 8), ("cnt", 16), ("ldp", 16),
    ("wy", 12), ("wz", 4), ("ry", 4), ("rx", 16), ("s2y", 4), ("s2x", 4),
    ("s3", 8), ("agz", 4), ("agx", 8),
)


def kernel(
    hid, tea, w, info, loss_o, gain_o, key_o,
    hbuf, tbuf, wbuf, nbuf, inv, keys, dkt, gbuf, ry, rx, s2y, sx, r2y, r2x, t3, r3,
    fin, kt, outs, isib, gfull, cbuf, lown, lsib, lsh, ldp,
    lsem, ssem, rsem, zsem,
):
    zl, x = lax.axis_index("dp_0"), lax.axis_index("dp_1")
    h, y, c = (lax.axis_index(a) for a in SHARD)

    def ring4(v, d):
        return lax.rem(v + d, 4)

    def to_y(d):
        return {"shard_1": ring4(y, d)}

    def to_x(d):
        return {"dp_1": ring4(x, d)}

    sib = {"shard_2": 1 - c}

    def send(src, dst, slot, dev):
        return pltpu.make_async_remote_copy(
            src_ref=src, dst_ref=dst, send_sem=ssem.at[slot], recv_sem=rsem.at[slot],
            device_id=dev, device_id_type=MESH,
        )

    shard_peers = [
        (dh * 4 + dy, {"shard_0": lax.rem(h + dh, 2), "shard_1": ring4(y, dy)})
        for dh in range(2) for dy in range(4) if dh or dy
    ]
    dp_peers = [
        (dl * 4 + dx, {"dp_0": ring4(zl, dl), "dp_1": ring4(x, dx)})
        for dl in range(4) for dx in range(4) if dl or dx
    ]
    z_peers = [
        (dh * 4 + dl, {"shard_0": lax.rem(h + dh, 2), "dp_0": ring4(zl, dl)})
        for dh in range(2) for dl in range(4) if dh or dl
    ]
    extra = [dev for at, dev in z_peers if at > 4]
    everyone = [sib] + [dev for _, dev in shard_peers + dp_peers] + extra

    own_rows = pl.ds(pl.multiple_of(h * PC + c * SL, 64), SL)
    my_cols = pl.ds(pl.multiple_of(c * HK, 128), HK)
    sib_cols = pl.ds(pl.multiple_of((1 - c) * HK, 128), HK)
    mine = y * 2 + h
    gid = zl * 4 + x

    own_hid = pltpu.make_async_copy(hid, hbuf.at[c], lsem.at[0])
    own_hid.start()
    own_w = pltpu.make_async_copy(w.at[:, my_cols], wbuf.at[y, own_rows], lsem.at[1])
    own_w.start()
    own_tea = pltpu.make_async_copy(tea.at[:, my_cols], tbuf.at[c], lsem.at[2])
    own_tea.start()

    barrier = pltpu.get_barrier_semaphore()
    for dev in everyone:
        pl.semaphore_signal(barrier, inc=1, device_id=dev, device_id_type=MESH)
    pl.semaphore_wait(barrier, len(everyone))

    sib_w = send(w.at[:, sib_cols], wbuf.at[y, own_rows], SLOT["w"], sib)
    sib_w.start()
    sib_info = send(info, isib, SLOT["info"], sib)
    sib_info.start()
    sib_tea = send(tea.at[:, sib_cols], tbuf.at[c], SLOT["tea"], sib)
    sib_tea.start()
    sib_hid = send(hid, hbuf.at[c], SLOT["hid"], sib)
    sib_hid.start()

    edge = (zl == 0) | (zl == 3)
    over = {"shard_0": 1 - h, "dp_0": 3 - zl}
    inner = {"dp_0": jnp.where(zl == 0, 1, 2)}
    zrows = PC // 4

    def z_piece(half, i):
        return wbuf.at[y, pl.ds(pl.multiple_of(half * PC + i * zrows, 32), zrows)]

    def z_over(i):
        return send(z_piece(h, i), z_piece(h, i), SLOT["wz"] + i, over)

    def z_in(i):
        ref = z_piece(1 - h, i)
        return pltpu.make_async_remote_copy(
            src_ref=ref, dst_ref=ref, send_sem=zsem.at[i], recv_sem=rsem.at[SLOT["wz"] + i],
            device_id=inner, device_id_type=MESH,
        )

    def y_copies(g):
        half = h if g == 0 else 1 - h
        base = SLOT["wy"] + 6 * g

        def part(owner, b):
            return wbuf.at[owner, pl.ds(pl.multiple_of(half * PC + b * SL, 64), SL)]

        def copy(owner, b, d, i):
            return send(part(owner, b), part(owner, b), base + i, to_y(d))

        return [
            copy(y, 0, 1, 0), copy(y, 1, 3, 1), copy(y, 1, 1, 2), copy(y, 0, 3, 3),
            copy(ring4(y, 3), 0, 1, 4), copy(ring4(y, 1), 1, 3, 5),
        ]

    first, second = y_copies(0), y_copies(1)
    own_w.wait()
    sib_w.wait_recv()

    @pl.when(edge)
    def _():
        for i in range(4):
            z_over(i).start()

    for copy in first[:4]:
        copy.start()

    sib_info.wait_recv()
    gfull[mine] = info[...] + isib[...]
    gsend = [
        send(gfull.at[mine], gfull.at[mine], SLOT["ginfo"] + at, dev) for at, dev in shard_peers
    ]
    for copy in gsend:
        copy.start()

    def norms(which):
        @pl.loop(0, TOK // 32)
        def _(i):
            rows = pl.ds(pl.multiple_of(i * 32, 32), 32)
            v = hbuf[which, rows, :].astype(F32)
            mean = jnp.sum(v * v, axis=1, keepdims=True) * (1.0 / D)
            inv[which, rows, :] = jnp.broadcast_to(lax.rsqrt(mean + EPSILON), (32, 128))

    own_hid.wait()
    norms(c)
    for copy in gsend:
        copy.wait_recv()
    group = gfull[0, :, 0:128]
    for i in range(1, 8):
        group = group + gfull[i, :, 0:128]
    cbuf[gid] = group
    csend = [send(cbuf.at[gid], cbuf.at[gid], SLOT["cnt"] + at, dev) for at, dev in dp_peers]
    for copy in csend:
        copy.start()
    sib_hid.wait_recv()
    norms(1 - c)

    for yy in range(4):
        for hh in range(2):
            src = (hh * 4 + yy) * PC
            dst = (yy * 2 + hh) * PC
            gain = gfull[yy * 2 + hh, 0:1, :]
            for which in range(2):
                @pl.loop(0, TOK // 32)
                def _(i):
                    rows = pl.ds(pl.multiple_of(i * 32, 32), 32)
                    out = pl.ds(pl.multiple_of(which * TOK + i * 32, 32), 32)
                    v = hbuf[which, rows, src : src + PC].astype(F32)
                    nbuf[out, dst : dst + PC] = (v * inv[which, rows, 0:1] * gain).astype(BF16)

    def project(owner, half, start=False):
        cols = pl.ds(pl.multiple_of(owner * YB + half * PC, 128), PC)
        rows = pl.ds(pl.multiple_of(half * PC, 64), PC)
        part = jnp.dot(nbuf[:, cols], wbuf[owner, rows, :], preferred_element_type=F32)
        keys[...] = part if start else keys[...] + part

    def y_steps(copies, half):
        copies[0].wait_recv()
        copies[4].start()
        copies[1].wait_recv()
        copies[5].start()
        copies[2].wait_recv()
        copies[3].wait_recv()

    y_steps(first, h)
    project(y, h, True)
    project(ring4(y, 3), h)
    project(ring4(y, 1), h)
    first[4].wait_recv()
    first[5].wait_recv()
    project(ring4(y, 2), h)

    for i in range(4):
        z_in(i).wait_recv()

        @pl.when(edge)
        def _():
            z_in(i).start()

    for copy in second[:4]:
        copy.start()
    project(y, 1 - h)
    y_steps(second, 1 - h)
    project(ring4(y, 3), 1 - h)
    project(ring4(y, 1), 1 - h)
    for copy in csend:
        copy.wait_recv()
    second[4].wait_recv()
    second[5].wait_recv()
    project(ring4(y, 2), 1 - h)

    count = cbuf[0]
    for i in range(1, 16):
        count = count + cbuf[i]
    count = count[1:2, 0:1]
    scale = SCALE / count
    sib_tea.wait_recv()
    own_tea.wait()
    own_n = info[1:2, 0:1]
    sib_n = isib[1:2, 0:1]
    position = lax.broadcasted_iota(jnp.int32, (TOK, 1), 0).astype(F32)
    squares = jnp.zeros((1, HK), F32)
    for which in range(2):
        live = jnp.where(c == which, own_n, sib_n)
        valid = jnp.where(position < live, 1.0, 0.0)
        rows = slice(which * TOK, (which + 1) * TOK)
        diff = keys[rows, :] - tbuf[which].astype(F32)
        squares = squares + jnp.sum(valid * diff * diff, axis=0, keepdims=True)
        dk = scale * valid * diff
        dkt[:, rows] = jnp.transpose(dk).astype(BF16)
    lown[...] = jnp.broadcast_to(jnp.sum(squares, axis=1, keepdims=True), (8, 128))
    lsend = send(lown, lsib, SLOT["lsib"], sib)
    lsend.start()

    stage1 = []
    for j in (1, 3, 2, 0):
        yy = ring4(y, j)
        cols = pl.ds(pl.multiple_of(yy * YB, 128), YB)
        gbuf[yy] = jnp.dot(dkt[...], nbuf[:, cols], preferred_element_type=F32).astype(BF16)
        if j:
            copy = send(gbuf.at[yy, 0:QK], ry.at[j - 1], SLOT["ry"] + j, to_y(j))
            copy.start()
            stage1.append(copy)
        for i in (1, 3, 2):
            rows = pl.ds(pl.multiple_of(QK + XK * ring4(x, i), 16), XK)
            copy = send(
                gbuf.at[yy, rows], rx.at[i - 1, yy], SLOT["rx"] + 4 * i + j, to_x(i)
            )
            copy.start()
            stage1.append(copy)

    lsend.wait_recv()
    lsh[mine] = lown[...] + lsib[...]
    lsends = [send(lsh.at[mine], lsh.at[mine], SLOT["lsh"] + at, dev) for at, dev in shard_peers]
    for copy in lsends:
        copy.start()

    for copy in stage1:
        copy.wait_recv()

    stage2 = []
    s2y[...] = (
        gbuf[y, 0:QK].astype(F32) + ry[0].astype(F32) + ry[1].astype(F32) + ry[2].astype(F32)
    )
    for i in (1, 3, 2):
        rows = pl.ds(pl.multiple_of(XK * ring4(x, i), 16), XK)
        copy = send(s2y.at[rows], r2y.at[i - 1], SLOT["s2y"] + i, to_x(i))
        copy.start()
        stage2.append(copy)
    my_x = pl.ds(pl.multiple_of(QK + XK * x, 16), XK)
    for j in (1, 3, 2, 0):
        yy = ring4(y, j)
        sx[yy] = (
            gbuf[yy, my_x, :].astype(F32)
            + rx[0, yy].astype(F32) + rx[1, yy].astype(F32) + rx[2, yy].astype(F32)
        )
        if j:
            copy = send(sx.at[yy], r2x.at[j - 1], SLOT["s2x"] + j, to_y(j))
            copy.start()
            stage2.append(copy)

    for copy in lsends:
        copy.wait_recv()
    total = lsh[0]
    for i in range(1, 8):
        total = total + lsh[i]
    ldp[gid] = total
    lsends2 = [send(ldp.at[gid], ldp.at[gid], SLOT["ldp"] + at, dev) for at, dev in dp_peers]
    for copy in lsends2:
        copy.start()

    for copy in stage2:
        copy.wait_recv()
    upper = s2y[pl.ds(pl.multiple_of(XK * x, 16), XK), :] + r2y[0] + r2y[1] + r2y[2]
    lower = sx[y] + r2x[0] + r2x[1] + r2x[2]
    for hh in range(2):
        for l in range(4):
            part = upper if l < 2 else lower
            t3[hh, l] = part[24 * (l % 2) : 24 * (l % 2) + 24, hh * PC : (hh + 1) * PC]
    stage3 = []
    for at, dev in z_peers:
        dh, dl = at // 4, at % 4
        copy = send(
            t3.at[lax.rem(h + dh, 2), ring4(zl, dl)], r3.at[at], SLOT["s3"] + at, dev
        )
        copy.start()
        stage3.append(copy)
    for copy in stage3:
        copy.wait_recv()
    piece = t3[h, zl]
    for at in range(1, 8):
        piece = piece + r3[at]
    fin[x, zl] = piece

    agz = [
        send(fin.at[x, zl], fin.at[x, zl], SLOT["agz"] + d, {"dp_0": ring4(zl, d)})
        for d in (1, 3, 2)
    ]
    for copy in agz:
        copy.start()
    for copy in agz:
        copy.wait_recv()
    agx = [send(fin.at[x], fin.at[x], SLOT["agx"] + d, to_x(d)) for d in (1, 3, 2)]
    for copy in agx:
        copy.start()

    for copy in lsends2:
        copy.wait_recv()
    total = ldp[0]
    for i in range(1, 16):
        total = total + ldp[i]
    loss_o[...] = total / (2.0 * KV * count)

    for copy in agx:
        copy.wait_recv()
    ordered = []
    for side in range(2):
        for xx in range(4):
            ordered += [fin[xx, 2 * side], fin[xx, 2 * side + 1]]
    kt[...] = jnp.transpose(jnp.concatenate(ordered, axis=0))
    osend = send(
        kt.at[pl.ds(pl.multiple_of((1 - c) * SL, 64), SL)], outs.at[:, my_cols],
        SLOT["out"], sib,
    )
    osend.start()
    own_out = pltpu.make_async_copy(
        kt.at[pl.ds(pl.multiple_of(c * SL, 64), SL)], outs.at[:, my_cols], lsem.at[3]
    )
    own_out.start()
    own_out.wait()
    osend.wait_recv()
    key_out = pltpu.make_async_copy(outs, key_o, lsem.at[4])
    key_out.start()
    terms = outs[...] * w[...].astype(F32)
    gain_o[...] = lax.dot_general(
        jnp.ones((8, KV), F32), terms, (((1,), (1,)), ((), ())),
        preferred_element_type=F32, precision=lax.Precision.HIGHEST,
    )
    key_out.wait()

    for copy in (
        [sib_w, sib_info, sib_tea, sib_hid, lsend, osend] + first + second + gsend + csend
        + stage1 + lsends + stage2 + lsends2 + stage3 + agz + agx
    ):
        copy.wait_send()

    @pl.when(edge)
    def _():
        for i in range(4):
            z_over(i).wait_send()
            z_in(i).wait_send()


def body(hidden_in, teacher, norm_gain, w_key, group_rows, member):
    core = lax.axis_index("shard_2")
    gain = norm_gain.astype(F32)
    row = lax.broadcasted_iota(jnp.int32, (8, PC), 0)
    lane = lax.broadcasted_iota(jnp.int32, (8, PC), 1)
    own = (row == 0) & (lane >= core * SL) & (lane < core * SL + SL)
    live = (member[0, 0] * group_rows[0]).astype(F32)
    info = jnp.where(own, jnp.concatenate([gain, gain])[None, :], jnp.where(row == 1, live, 0.0))
    vm = pl.BlockSpec(memory_space=pltpu.VMEM)
    hbm = pl.BlockSpec(memory_space=pl.ANY)
    loss, gain_sum, grad_key = pl.pallas_call(
        kernel,
        out_shape=(
            jax.ShapeDtypeStruct((8, 128), F32),
            jax.ShapeDtypeStruct((8, SL), F32),
            jax.ShapeDtypeStruct((SL, KV), F32),
        ),
        in_specs=[hbm, vm, vm, vm],
        out_specs=(vm, vm, hbm),
        scratch_shapes=[
            pltpu.VMEM((2, TOK, D), BF16),
            pltpu.VMEM((2, TOK, HK), BF16),
            pltpu.VMEM((4, YB, HK), BF16),
            pltpu.VMEM((2 * TOK, D), BF16),
            pltpu.VMEM((2, TOK, 128), F32),
            pltpu.VMEM((2 * TOK, HK), F32),
            pltpu.VMEM((HK, 2 * TOK), BF16),
            pltpu.VMEM((4, HK, YB), BF16),
            pltpu.VMEM((3, QK, YB), BF16),
            pltpu.VMEM((3, 4, XK, YB), BF16),
            pltpu.VMEM((QK, YB), F32),
            pltpu.VMEM((4, XK, YB), F32),
            pltpu.VMEM((3, XK, YB), F32),
            pltpu.VMEM((3, XK, YB), F32),
            pltpu.VMEM((2, 4, 24, PC), F32),
            pltpu.VMEM((8, 24, PC), F32),
            pltpu.VMEM((4, 4, 24, PC), F32),
            pltpu.VMEM((PC, HK), F32),
            pltpu.VMEM((SL, KV), F32),
            pltpu.VMEM((8, PC), F32),
            pltpu.VMEM((8, 8, PC), F32),
            pltpu.VMEM((16, 8, 128), F32),
            pltpu.VMEM((8, 128), F32),
            pltpu.VMEM((8, 128), F32),
            pltpu.VMEM((8, 8, 128), F32),
            pltpu.VMEM((16, 8, 128), F32),
            pltpu.SemaphoreType.DMA((5,)),
            pltpu.SemaphoreType.DMA((N_SLOT,)),
            pltpu.SemaphoreType.DMA((N_SLOT,)),
            pltpu.SemaphoreType.DMA((4,)),
        ],
        compiler_params=pltpu.CompilerParams(
            collective_id=0, has_side_effects=True, vmem_limit_bytes=62 * 2**20
        ),
    )(hidden_in, teacher, w_key, info)
    return loss[0, 0], gain_sum[0] / gain, grad_key


def solution(mesh):
    split = Mesh(mesh.devices.reshape(4, 4, 2, 4, 2), DP_SHARD)
    return jax.shard_map(
        body,
        mesh=split,
        in_specs=(
            P(DP_SHARD, None),
            P(DP_SHARD, None),
            P(SHARD),
            P(SHARD, None),
            P(DP),
            P(DP, SHARD),
        ),
        out_specs=(P(), P(SHARD), P(SHARD, None)),
        check_vma=False,
    )
```

time: 396 us -> 156 us (0.39)
  waiting for transfers between devices: 236 us -> 0 us
  Pallas kernels: 0 us -> 148 us
  blocking collectives: 79.2 us -> 0 us
  matrix products: 21.5 us -> 0 us
  between operations: 18.5 us -> 1.98 us
  starting transfers between devices: 12.8 us -> 0 us
  other arithmetic: 11.3 us -> 2.05 us
  local copies, waits for them, and re-layouts: 13.3 us -> 4.14 us
    pallas_call x0 -> x1, Pallas kernels: none -> 148 us  [body(): pl.pallas_call(kernel, out_shape=(jax.ShapeDtypeStruct((8, 128), F32), ja...]
    all_to_all x3 -> x0, waiting for transfers between devices: 122 us -> none  [the longest x1 94.4 us: body(): lax.all_to_all(normed, SHARD, split_axis=1, concat_axis=0, tiled=True)]
    all_gather x2 -> x0, waiting for transfers between devices: 115 us -> none  [the longest x1 113 us: in_one_piece(): lax.all_gather(both, axis, axis=dim, tiled=True)]
    psum x5 -> x0, blocking collectives: 45.1 us -> none  [over_axes(): return functools.reduce(lax.psum, axes, value)]
    all_to_all x1 -> x0, blocking collectives: 34.1 us -> none  [summed_on_arrival(): lax.all_to_all(blocks, axis, split_axis=0, concat_axis=0, tiled=True)]
    dot_general x3 -> x0, matrix products: 21.5 us -> none  [the longest x1 8.52 us: body(): keys = jnp.dot(normed, key_full, preferred_element_type=jnp.float32)]
    all_to_all x3 -> x0, starting transfers between devices: 12.7 us -> none  [the longest x1 5.18 us: from_everyone(): return lax.all_to_all(copies, axis, split_axis=0, concat_axis=0, tiled=True)]
    convert_element_type x1 -> x0, local copies, waits for them, and re-layouts: 4.39 us -> none  [body(): normed = (scaled * gains.astype(jnp.float32)).astype(jnp.bfloat16)]
  transfers between devices with their start and end apart: 5 -> 0, of which waited for: 5 -> 0; matrix products, arithmetic and copies ran while one was open for 4% -> 0% of each run, Pallas kernels for 0% -> 0%
where the time goes in v1:
time: 156 us
  Pallas kernels  148 us (95%)
  local copies, waits for them, and re-layouts  4.14 us (3%)
  other arithmetic  2.05 us (1%)
  between operations  1.98 us (1%)
    pallas_call x1, Pallas kernels, body(): pl.pallas_call(kernel, out_shape=(jax.ShapeDtypeStruct((8, 128), F32), ja...  148 us

profile of v1, /device:TPU:1, one launch (start us, length us, event | category | flops | bytes accessed | tf_op | source)
XLA Modules:
  0.0 156.0 jit_solution(3714023796894919370)
XLA Ops:
  0.6 0.0 copy-start
  2.0 0.7 convert_element_type.6
  2.7 0.1 pad_maximum_fusion
  2.7 0.7 and_select_fusion.info
  3.4 147.8 %shard_map.85 = (f32[8,128]{1,0:T(8,128)}, f32[8,320]{1,0:T(8,128)}, f32[320,768]{1,0:T(8,128)}) custom-call(bf16[256,5120]{1,0:T(8,128)(2,1)} %hid.1, bf16[256,768]{1,0:T(8,128)(2,1)} %tea.1, bf16[320,768]{1,0:T(8,128)(2,1)} %w.1, f32[8,640]{1,0:T(8,128)} %and_select_fusion.info), custom_call_target="tpu_custom_call" | custom-call | tf_op jit(solution)/shard_map/pallas_call | solution.py:416
  151.2 1.2 slice.6
  152.4 0.7 slice_reduce_fusion
  153.2 0.0 copy-done
  153.2 0.6 convert_divide_fusion
  153.7 2.2 %copy.12 = f32[320,768]{1,0:T(8,128)} copy(f32[320,768]{1,0:T(8,128)} %get-tuple-element.16) | data formatting | bytes 1966080
  (3 shorter events, 0.0 us)
Async XLA Ops:
  0.6 152.5 %copy-start = (bf16[320]{0:T(512)(128)(2,1)S(1)}, bf16[320]{0:T(512)(128)(2,1)}, u32[]{:S(2)}) copy-start(bf16[320]{0:T(512)(128)(2,1)} %param.8) | copy-start | bytes 1924

commit v2 on v1

--- a/solution.py
+++ b/solution.py
@@ -25,6 +25,10 @@
 QK = HK // 2
 XK = QK // 4
 
+DR = 160
+SR = 80
+SA = 48
+
 SMALL = ("info", "w", "tea", "hid", "lsib", "out")
 
 
@@ -39,13 +43,13 @@
 SLOT, N_SLOT = slots(
     *((name, 1) for name in SMALL),
     ("ginfo", 8), ("lsh", 8), ("cnt", 16), ("ldp", 16),
-    ("wy", 12), ("wz", 4), ("ry", 4), ("rx", 16), ("s2y", 4), ("s2x", 4),
+    ("wy", 20), ("wx", 32), ("wz", 3), ("ry", 4), ("rx", 16), ("s2y", 4), ("s2x", 4),
     ("s3", 8), ("agz", 4), ("agx", 8),
 )
 
 
 def kernel(
-    hid, tea, w, info, loss_o, gain_o, key_o,
+    hid, tea, w, gain, info, loss_o, gain_o, key_o,
     hbuf, tbuf, wbuf, nbuf, inv, keys, dkt, gbuf, ry, rx, s2y, sx, r2y, r2x, t3, r3,
     fin, kt, outs, isib, gfull, cbuf, lown, lsib, lsh, ldp,
     lsem, ssem, rsem, zsem,
@@ -115,55 +119,85 @@
     edge = (zl == 0) | (zl == 3)
     over = {"shard_0": 1 - h, "dp_0": 3 - zl}
     inner = {"dp_0": jnp.where(zl == 0, 1, 2)}
-    zrows = PC // 4
-
-    def z_piece(half, i):
-        return wbuf.at[y, pl.ds(pl.multiple_of(half * PC + i * zrows, 32), zrows)]
+    split = PC // 2 + SR * x
+
+    def part(owner, half, at, n):
+        return wbuf.at[owner, pl.ds(pl.multiple_of(half * PC + at, 16), n)]
+
+    z_parts = ((split, SR), (0, DR), (DR, DR))
 
     def z_over(i):
-        return send(z_piece(h, i), z_piece(h, i), SLOT["wz"] + i, over)
+        ref = part(y, h, *z_parts[i])
+        return send(ref, ref, SLOT["wz"] + i, over)
 
     def z_in(i):
-        ref = z_piece(1 - h, i)
+        ref = part(y, 1 - h, *z_parts[i])
         return pltpu.make_async_remote_copy(
             src_ref=ref, dst_ref=ref, send_sem=zsem.at[i], recv_sem=rsem.at[SLOT["wz"] + i],
             device_id=inner, device_id_type=MESH,
         )
 
+    def z_take(i):
+        z_in(i).wait_recv()
+
+        @pl.when(edge)
+        def _():
+            z_in(i).start()
+
     def y_copies(g):
         half = h if g == 0 else 1 - h
-        base = SLOT["wy"] + 6 * g
-
-        def part(owner, b):
-            return wbuf.at[owner, pl.ds(pl.multiple_of(half * PC + b * SL, 64), SL)]
-
-        def copy(owner, b, d, i):
-            return send(part(owner, b), part(owner, b), base + i, to_y(d))
-
-        return [
-            copy(y, 0, 1, 0), copy(y, 1, 3, 1), copy(y, 1, 1, 2), copy(y, 0, 3, 3),
-            copy(ring4(y, 3), 0, 1, 4), copy(ring4(y, 1), 1, 3, 5),
+        back, ahead = ring4(y, 3), ring4(y, 1)
+        plan = (
+            (y, split, SR, 1), (y, split, SR, 3),
+            (y, 0, DR, 1), (y, DR, DR, 3), (y, DR, DR, 1), (y, 0, DR, 3),
+            (back, split, SA, 1), (ahead, split + SA, SR - SA, 3),
+            (back, 0, DR, 1), (ahead, DR, DR, 3),
+        )
+        copies = []
+        for i, (owner, at, n, d) in enumerate(plan):
+            ref = part(owner, half, at, n)
+            copies.append(send(ref, ref, SLOT["wy"] + 10 * g + i, to_y(d)))
+        return copies
+
+    first, second = y_copies(0), y_copies(1)
+    handed = {}
+
+    def hand(g, k):
+        ref = part(ring4(y, k), h if g == 0 else 1 - h, split, SR)
+        handed[g, k] = [
+            send(ref, ref, SLOT["wx"] + 16 * g + 4 * k + i, to_x(i)) for i in (1, 3, 2)
         ]
-
-    first, second = y_copies(0), y_copies(1)
-    own_w.wait()
-    sib_w.wait_recv()
-
-    @pl.when(edge)
-    def _():
-        for i in range(4):
-            z_over(i).start()
-
-    for copy in first[:4]:
-        copy.start()
+        for copy in handed[g, k]:
+            copy.start()
+
+    def take(*copies):
+        for copy in copies:
+            copy.wait_recv()
+
+    def go(*copies):
+        for copy in copies:
+            copy.start()
 
     sib_info.wait_recv()
     gfull[mine] = info[...] + isib[...]
     gsend = [
         send(gfull.at[mine], gfull.at[mine], SLOT["ginfo"] + at, dev) for at, dev in shard_peers
     ]
-    for copy in gsend:
-        copy.start()
+    go(*gsend)
+    own_w.wait()
+    sib_w.wait_recv()
+    go(first[0], first[1])
+
+    @pl.when(edge)
+    def _():
+        z_over(0).start()
+
+    go(first[2], first[3])
+
+    @pl.when(edge)
+    def _():
+        z_over(1).start()
+        z_over(2).start()
 
     def norms(which):
         @pl.loop(0, TOK // 32)
@@ -173,73 +207,87 @@
             mean = jnp.sum(v * v, axis=1, keepdims=True) * (1.0 / D)
             inv[which, rows, :] = jnp.broadcast_to(lax.rsqrt(mean + EPSILON), (32, 128))
 
+    def normalize(yy, hh):
+        src = (hh * 4 + yy) * PC
+        dst = (yy * 2 + hh) * PC
+        for which in range(2):
+            @pl.loop(0, TOK // 64)
+            def _(i):
+                rows = pl.ds(pl.multiple_of(i * 64, 64), 64)
+                out = pl.ds(pl.multiple_of(which * TOK + i * 64, 64), 64)
+                scale = inv[which, rows, :]
+                for lane in range(0, PC, 128):
+                    by = gfull[yy * 2 + hh, 0:1, lane : lane + 128]
+                    v = hbuf[which, rows, src + lane : src + lane + 128].astype(F32)
+                    nbuf[out, dst + lane : dst + lane + 128] = (v * scale * by).astype(BF16)
+
+    def project(k, g, start=False):
+        half = h if g == 0 else 1 - h
+        owner = ring4(y, k)
+        cols = pl.ds(pl.multiple_of(owner * YB + half * PC, 128), PC)
+        rows = pl.ds(pl.multiple_of(half * PC, 64), PC)
+        term = jnp.dot(nbuf[:, cols], wbuf[owner, rows, :], preferred_element_type=F32)
+        keys[...] = term if start else keys[...] + term
+
     own_hid.wait()
     norms(c)
-    for copy in gsend:
-        copy.wait_recv()
+    take(first[0], first[1])
+    go(first[6], first[7])
+    hand(0, 3)
+    hand(0, 1)
+    go(first[4], first[5])
+    z_take(0)
+    go(second[0], second[1])
+    hand(1, 0)
+    take(*gsend)
     group = gfull[0, :, 0:128]
     for i in range(1, 8):
         group = group + gfull[i, :, 0:128]
     cbuf[gid] = group
     csend = [send(cbuf.at[gid], cbuf.at[gid], SLOT["cnt"] + at, dev) for at, dev in dp_peers]
-    for copy in csend:
-        copy.start()
+    go(*csend)
     sib_hid.wait_recv()
     norms(1 - c)
-
-    for yy in range(4):
-        for hh in range(2):
-            src = (hh * 4 + yy) * PC
-            dst = (yy * 2 + hh) * PC
-            gain = gfull[yy * 2 + hh, 0:1, :]
-            for which in range(2):
-                @pl.loop(0, TOK // 32)
-                def _(i):
-                    rows = pl.ds(pl.multiple_of(i * 32, 32), 32)
-                    out = pl.ds(pl.multiple_of(which * TOK + i * 32, 32), 32)
-                    v = hbuf[which, rows, src : src + PC].astype(F32)
-                    nbuf[out, dst : dst + PC] = (v * inv[which, rows, 0:1] * gain).astype(BF16)
-
-    def project(owner, half, start=False):
-        cols = pl.ds(pl.multiple_of(owner * YB + half * PC, 128), PC)
-        rows = pl.ds(pl.multiple_of(half * PC, 64), PC)
-        part = jnp.dot(nbuf[:, cols], wbuf[owner, rows, :], preferred_element_type=F32)
-        keys[...] = part if start else keys[...] + part
-
-    def y_steps(copies, half):
-        copies[0].wait_recv()
-        copies[4].start()
-        copies[1].wait_recv()
-        copies[5].start()
-        copies[2].wait_recv()
-        copies[3].wait_recv()
-
-    y_steps(first, h)
-    project(y, h, True)
-    project(ring4(y, 3), h)
-    project(ring4(y, 1), h)
-    first[4].wait_recv()
-    first[5].wait_recv()
-    project(ring4(y, 2), h)
-
-    for i in range(4):
-        z_in(i).wait_recv()
-
-        @pl.when(edge)
-        def _():
-            z_in(i).start()
-
-    for copy in second[:4]:
-        copy.start()
-    project(y, 1 - h)
-    y_steps(second, 1 - h)
-    project(ring4(y, 3), 1 - h)
-    project(ring4(y, 1), 1 - h)
-    for copy in csend:
-        copy.wait_recv()
-    second[4].wait_recv()
-    second[5].wait_recv()
-    project(ring4(y, 2), 1 - h)
+    take(first[2], first[3])
+    go(first[8], first[9])
+    z_take(1)
+    go(second[2], second[5])
+    normalize(0, 0)
+    take(second[0], second[1])
+    go(second[6], second[7])
+    hand(1, 3)
+    hand(1, 1)
+    normalize(0, 1)
+    take(first[6], first[7])
+    hand(0, 2)
+    normalize(1, 0)
+    z_take(2)
+    go(second[3], second[4])
+    normalize(1, 1)
+    normalize(2, 0)
+    take(second[2])
+    go(second[8])
+    take(second[6], second[7])
+    hand(1, 2)
+    normalize(2, 1)
+    normalize(3, 0)
+    normalize(3, 1)
+    take(second[3])
+    go(second[9])
+    project(0, 0, True)
+    take(*handed[0, 3], *handed[0, 1], first[4], first[5])
+    project(3, 0)
+    project(1, 0)
+    take(*handed[1, 0])
+    project(0, 1)
+    take(*handed[0, 2], first[8], first[9])
+    project(2, 0)
+    take(*csend)
+    take(*handed[1, 3], *handed[1, 1], second[4], second[5])
+    project(3, 1)
+    project(1, 1)
+    take(*handed[1, 2], second[8], second[9])
+    project(2, 1)
 
     count = cbuf[0]
     for i in range(1, 16):
@@ -327,8 +375,8 @@
     lower = sx[y] + r2x[0] + r2x[1] + r2x[2]
     for hh in range(2):
         for l in range(4):
-            part = upper if l < 2 else lower
-            t3[hh, l] = part[24 * (l % 2) : 24 * (l % 2) + 24, hh * PC : (hh + 1) * PC]
+            rows = upper if l < 2 else lower
+            t3[hh, l] = rows[24 * (l % 2) : 24 * (l % 2) + 24, hh * PC : (hh + 1) * PC]
     stage3 = []
     for at, dev in z_peers:
         dh, dl = at // 4, at % 4
@@ -342,7 +390,7 @@
     piece = t3[h, zl]
     for at in range(1, 8):
         piece = piece + r3[at]
-    fin[x, zl] = piece
+    fin[x, zl] = piece.astype(BF16)
 
     agz = [
         send(fin.at[x, zl], fin.at[x, zl], SLOT["agz"] + d, {"dp_0": ring4(zl, d)})
@@ -361,14 +409,14 @@
     total = ldp[0]
     for i in range(1, 16):
         total = total + ldp[i]
-    loss_o[...] = total / (2.0 * KV * count)
+    loss_o[...] = (total / (2.0 * KV * count))[0:1, 0:1]
 
     for copy in agx:
         copy.wait_recv()
     ordered = []
     for side in range(2):
         for xx in range(4):
-            ordered += [fin[xx, 2 * side], fin[xx, 2 * side + 1]]
+            ordered += [fin[xx, 2 * side + l].astype(F32) for l in range(2)]
     kt[...] = jnp.transpose(jnp.concatenate(ordered, axis=0))
     osend = send(
         kt.at[pl.ds(pl.multiple_of((1 - c) * SL, 64), SL)], outs.at[:, my_cols],
@@ -384,21 +432,22 @@
     key_out = pltpu.make_async_copy(outs, key_o, lsem.at[4])
     key_out.start()
     terms = outs[...] * w[...].astype(F32)
-    gain_o[...] = lax.dot_general(
+    summed = lax.dot_general(
         jnp.ones((8, KV), F32), terms, (((1,), (1,)), ((), ())),
         preferred_element_type=F32, precision=lax.Precision.HIGHEST,
     )
+    gain_o[...] = summed[0:1, :] / gain[...]
     key_out.wait()
 
     for copy in (
         [sib_w, sib_info, sib_tea, sib_hid, lsend, osend] + first + second + gsend + csend
-        + stage1 + lsends + stage2 + lsends2 + stage3 + agz + agx
+        + sum(handed.values(), []) + stage1 + lsends + stage2 + lsends2 + stage3 + agz + agx
     ):
         copy.wait_send()
 
     @pl.when(edge)
     def _():
-        for i in range(4):
+        for i in range(3):
             z_over(i).wait_send()
             z_in(i).wait_send()
 
@@ -413,14 +462,14 @@
     info = jnp.where(own, jnp.concatenate([gain, gain])[None, :], jnp.where(row == 1, live, 0.0))
     vm = pl.BlockSpec(memory_space=pltpu.VMEM)
     hbm = pl.BlockSpec(memory_space=pl.ANY)
-    loss, gain_sum, grad_key = pl.pallas_call(
+    loss, grad_gain, grad_key = pl.pallas_call(
         kernel,
         out_shape=(
-            jax.ShapeDtypeStruct((8, 128), F32),
-            jax.ShapeDtypeStruct((8, SL), F32),
+            jax.ShapeDtypeStruct((1, 1), F32),
+            jax.ShapeDtypeStruct((1, SL), F32),
             jax.ShapeDtypeStruct((SL, KV), F32),
         ),
-        in_specs=[hbm, vm, vm, vm],
+        in_specs=[hbm, vm, vm, vm, vm],
         out_specs=(vm, vm, hbm),
         scratch_shapes=[
             pltpu.VMEM((2, TOK, D), BF16),
@@ -439,7 +488,7 @@
             pltpu.VMEM((3, XK, YB), F32),
             pltpu.VMEM((2, 4, 24, PC), F32),
             pltpu.VMEM((8, 24, PC), F32),
-            pltpu.VMEM((4, 4, 24, PC), F32),
+            pltpu.VMEM((4, 4, 24, PC), BF16),
             pltpu.VMEM((PC, HK), F32),
             pltpu.VMEM((SL, KV), F32),
             pltpu.VMEM((8, PC), F32),
@@ -452,13 +501,13 @@
             pltpu.SemaphoreType.DMA((5,)),
             pltpu.SemaphoreType.DMA((N_SLOT,)),
             pltpu.SemaphoreType.DMA((N_SLOT,)),
-            pltpu.SemaphoreType.DMA((4,)),
+            pltpu.SemaphoreType.DMA((3,)),
         ],
         compiler_params=pltpu.CompilerParams(
             collective_id=0, has_side_effects=True, vmem_limit_bytes=62 * 2**20
         ),
-    )(hidden_in, teacher, w_key, info)
-    return loss[0, 0], gain_sum[0] / gain, grad_key
+    )(hidden_in, teacher, w_key, gain[None, :], info)
+    return loss.reshape(()), grad_gain.reshape(SL), grad_key
 
 
 def solution(mesh):

time: 156 us -> 120 us (0.77)
  Pallas kernels: 148 us -> 110 us
  between operations: 1.98 us -> 3.65 us
    pallas_call x1, Pallas kernels: 148 us -> 110 us  [body(): pl.pallas_call(kernel, out_shape=(jax.ShapeDtypeStruct((1, 1), F32), jax....]
    slice x2 -> x0, local copies, waits for them, and re-layouts: 1.92 us -> none  [body(): return (loss[0, 0], gain_sum[0] / gain, grad_key)]
where the time goes in v2:
time: 120 us
  Pallas kernels  110 us (92%)
  between operations  3.65 us (3%)
  local copies, waits for them, and re-layouts  3.45 us (3%)
  other arithmetic  2.72 us (2%)
    pallas_call x1, Pallas kernels, body(): pl.pallas_call(kernel, out_shape=(jax.ShapeDtypeStruct((1, 1), F32), jax....  110 us

profile of v2, /device:TPU:1, one launch (start us, length us, event | category | flops | bytes accessed | tf_op | source)
XLA Modules:
  0.0 119.8 jit_solution(17190141625054155888)
XLA Ops:
  0.6 0.7 convert_element_type.6
  1.3 0.1 pad_maximum_fusion
  2.7 0.7 and_select_fusion.info
  3.4 1.2 %broadcast_in_dim.20.gain = f32[1,320]{1,0:T(1,128)} reshape(bf16[320]{0:T(512)(128)(2,1)} %param.8) | data formatting | bytes 1920 | tf_op jit(solution)/shard_map/broadcast_in_dim | solution.py:509
  4.7 110.0 %shard_map.85 = (f32[1,1]{1,0:T(1,128)}, f32[1,320]{1,0:T(1,128)}, f32[320,768]{1,0:T(8,128)}) custom-call(bf16[256,5120]{1,0:T(8,128)(2,1)} %hid.1, bf16[256,768]{1,0:T(8,128)(2,1)} %tea.1, bf16[320,768]{1,0:T(8,128)(2,1)} %w.1, f32[1,320]{1,0:T(1,128)} %broadcast_in_dim.20.gain, f32[8,640]{1,0:T(8,128)} %and_select_fusion.info), custom_call_target="tpu_custom_call" | custom-call | tf_op jit(solution)/shard_map/pallas_call | solution.py:465
  114.7 1.3 %reduce = f32[320]{0:T(512)} reduce(f32[1,320]{1,0:T(1,128)} %get-tuple-element.7, f32[]{:T(128)} %constant.14), dimensions={0}, to_apply=%get-tuple-element.7.reduce_sub_computation | reduce | bytes 2564 | tf_op jit(solution)/shard_map/pallas_call | solution.py:465
  116.5 2.2 %copy.14 = f32[320,768]{1,0:T(8,128)} copy(f32[320,768]{1,0:T(8,128)} %get-tuple-element.16) | data formatting | bytes 1966080
  (3 shorter events, 0.0 us)

commit v3 on v2

--- a/solution.py
+++ b/solution.py
@@ -23,7 +23,10 @@
 PC = 2 * SL
 YB = 2 * PC
 QK = HK // 2
-XK = QK // 4
+CH = 3
+CK = QK // CH
+XK = CK // 4
+ZK = XK // 2
 
 DR = 160
 SR = 80
@@ -43,15 +46,15 @@
 SLOT, N_SLOT = slots(
     *((name, 1) for name in SMALL),
     ("ginfo", 8), ("lsh", 8), ("cnt", 16), ("ldp", 16),
-    ("wy", 20), ("wx", 32), ("wz", 3), ("ry", 4), ("rx", 16), ("s2y", 4), ("s2x", 4),
-    ("s3", 8), ("agz", 4), ("agx", 8),
+    ("wy", 20), ("wx", 32), ("wz", 3), ("ry", 4 * CH), ("rx", 4 * (CH + 3)), ("s2y", 4 * CH), ("s2x", 4 * CH),
+    ("s3", 8 * CH), ("agz", 4 * CH), ("agx", 4 * CH),
 )
 
 
 def kernel(
-    hid, tea, w, gain, info, loss_o, gain_o, key_o,
-    hbuf, tbuf, wbuf, nbuf, inv, keys, dkt, gbuf, ry, rx, s2y, sx, r2y, r2x, t3, r3,
-    fin, kt, outs, isib, gfull, cbuf, lown, lsib, lsh, ldp,
+    hid, tea, w, gain, rows_of, alive, loss_o, gain_o, key_o,
+    hbuf, tbuf, wbuf, nbuf, inv, keys, dkt, gup, glow, ry, rx, s2y, sx, r2y, r2x, t3, r3,
+    fin, kt, outs, info, isib, gfull, cbuf, lown, lsib, lsh, ldp,
     lsem, ssem, rsem, zsem,
 ):
     zl, x = lax.axis_index("dp_0"), lax.axis_index("dp_1")
@@ -102,6 +105,12 @@
     own_tea = pltpu.make_async_copy(tea.at[:, my_cols], tbuf.at[c], lsem.at[2])
     own_tea.start()
 
+    own_gain = gain[...].astype(F32).reshape(1, SL)
+    lane = lax.broadcasted_iota(jnp.int32, (1, PC), 1)
+    own = (lane >= c * SL) & (lane < c * SL + SL)
+    info[:, 0:PC] = jnp.where(own, jnp.concatenate([own_gain, own_gain], axis=1), 0.0)
+    info[:, PC:] = jnp.full((1, 128), (alive[0, 0] * rows_of[0]).astype(F32))
+
     barrier = pltpu.get_barrier_semaphore()
     for dev in everyone:
         pl.semaphore_signal(barrier, inc=1, device_id=dev, device_id_type=MESH)
@@ -217,7 +226,7 @@
                 out = pl.ds(pl.multiple_of(which * TOK + i * 64, 64), 64)
                 scale = inv[which, rows, :]
                 for lane in range(0, PC, 128):
-                    by = gfull[yy * 2 + hh, 0:1, lane : lane + 128]
+                    by = gfull[yy * 2 + hh, :, lane : lane + 128]
                     v = hbuf[which, rows, src + lane : src + lane + 128].astype(F32)
                     nbuf[out, dst + lane : dst + lane + 128] = (v * scale * by).astype(BF16)
 
@@ -240,9 +249,9 @@
     go(second[0], second[1])
     hand(1, 0)
     take(*gsend)
-    group = gfull[0, :, 0:128]
+    group = gfull[0, :, PC:]
     for i in range(1, 8):
-        group = group + gfull[i, :, 0:128]
+        group = group + gfull[i, :, PC:]
     cbuf[gid] = group
     csend = [send(cbuf.at[gid], cbuf.at[gid], SLOT["cnt"] + at, dev) for at, dev in dp_peers]
     go(*csend)
@@ -292,12 +301,12 @@
     count = cbuf[0]
     for i in range(1, 16):
         count = count + cbuf[i]
-    count = count[1:2, 0:1]
+    count = count[:, 0:1]
     scale = SCALE / count
     sib_tea.wait_recv()
     own_tea.wait()
-    own_n = info[1:2, 0:1]
-    sib_n = isib[1:2, 0:1]
+    own_n = info[:, PC : PC + 1]
+    sib_n = isib[:, PC : PC + 1]
     position = lax.broadcasted_iota(jnp.int32, (TOK, 1), 0).astype(F32)
     squares = jnp.zeros((1, HK), F32)
     for which in range(2):
@@ -308,116 +317,148 @@
         squares = squares + jnp.sum(valid * diff * diff, axis=0, keepdims=True)
         dk = scale * valid * diff
         dkt[:, rows] = jnp.transpose(dk).astype(BF16)
-    lown[...] = jnp.broadcast_to(jnp.sum(squares, axis=1, keepdims=True), (8, 128))
+    lown[...] = jnp.broadcast_to(jnp.sum(squares, axis=1, keepdims=True), (1, 128))
     lsend = send(lown, lsib, SLOT["lsib"], sib)
     lsend.start()
 
-    stage1 = []
+    def up_copy(i, j):
+        rows = pl.ds(CK * i, CK)
+        return send(
+            gup.at[ring4(y, j), rows], ry.at[j - 1, rows], SLOT["ry"] + CH * j + i, to_y(j)
+        )
+
+    def low_rows(i, xx):
+        return pl.ds(pl.multiple_of(CK * i + XK * xx, 16), XK)
+
+    stage1 = [[] for _ in range(CH)]
     for j in (1, 3, 2, 0):
         yy = ring4(y, j)
         cols = pl.ds(pl.multiple_of(yy * YB, 128), YB)
-        gbuf[yy] = jnp.dot(dkt[...], nbuf[:, cols], preferred_element_type=F32).astype(BF16)
+        term = jnp.dot(dkt[...], nbuf[:, cols], preferred_element_type=F32)
+        gup[yy] = term[:QK].astype(BF16)
+        glow[:, cols] = term[QK:].astype(BF16)
         if j:
-            copy = send(gbuf.at[yy, 0:QK], ry.at[j - 1], SLOT["ry"] + j, to_y(j))
-            copy.start()
-            stage1.append(copy)
-        for i in (1, 3, 2):
-            rows = pl.ds(pl.multiple_of(QK + XK * ring4(x, i), 16), XK)
+            stage1[0].append(up_copy(0, j))
+            stage1[0][-1].start()
+        for d in (1, 3, 2):
             copy = send(
-                gbuf.at[yy, rows], rx.at[i - 1, yy], SLOT["rx"] + 4 * i + j, to_x(i)
+                glow.at[low_rows(0, ring4(x, d)), cols], rx.at[d - 1, 0, :, cols],
+                SLOT["rx"] + 4 * j + d, to_x(d),
             )
             copy.start()
-            stage1.append(copy)
-
-    lsend.wait_recv()
+            stage1[0].append(copy)
+    for i in range(1, CH):
+        for d in (1, 3, 2):
+            stage1[i].append(up_copy(i, d))
+            stage1[i].append(send(
+                glow.at[low_rows(i, ring4(x, d))], rx.at[d - 1, i],
+                SLOT["rx"] + 4 * (3 + i) + d, to_x(d),
+            ))
+        go(*stage1[i])
+
+    take(lsend)
     lsh[mine] = lown[...] + lsib[...]
     lsends = [send(lsh.at[mine], lsh.at[mine], SLOT["lsh"] + at, dev) for at, dev in shard_peers]
-    for copy in lsends:
-        copy.start()
-
-    for copy in stage1:
-        copy.wait_recv()
-
-    stage2 = []
-    s2y[...] = (
-        gbuf[y, 0:QK].astype(F32) + ry[0].astype(F32) + ry[1].astype(F32) + ry[2].astype(F32)
-    )
-    for i in (1, 3, 2):
-        rows = pl.ds(pl.multiple_of(XK * ring4(x, i), 16), XK)
-        copy = send(s2y.at[rows], r2y.at[i - 1], SLOT["s2y"] + i, to_x(i))
-        copy.start()
-        stage2.append(copy)
-    my_x = pl.ds(pl.multiple_of(QK + XK * x, 16), XK)
-    for j in (1, 3, 2, 0):
-        yy = ring4(y, j)
-        sx[yy] = (
-            gbuf[yy, my_x, :].astype(F32)
-            + rx[0, yy].astype(F32) + rx[1, yy].astype(F32) + rx[2, yy].astype(F32)
+    go(*lsends)
+
+    stage2 = [[] for _ in range(CH)]
+    stage3 = [[] for _ in range(CH)]
+    agz = [[] for _ in range(CH)]
+    agx = [[] for _ in range(CH)]
+
+    def reduce1(i):
+        take(*stage1[i])
+        rows = slice(CK * i, CK * i + CK)
+        s2y[rows] = (
+            gup[y, rows].astype(F32) + ry[0, rows].astype(F32)
+            + ry[1, rows].astype(F32) + ry[2, rows].astype(F32)
         )
-        if j:
-            copy = send(sx.at[yy], r2x.at[j - 1], SLOT["s2x"] + j, to_y(j))
+        for d in (1, 3, 2):
+            stage2[i].append(
+                send(s2y.at[low_rows(i, ring4(x, d))], r2y.at[i, d - 1],
+                     SLOT["s2y"] + CH * d + i, to_x(d))
+            )
+            stage2[i][-1].start()
+        for j in (1, 3, 2, 0):
+            yy = ring4(y, j)
+            cols = pl.ds(pl.multiple_of(yy * YB, 128), YB)
+            sx[i, yy] = (
+                glow[low_rows(i, x), cols].astype(F32) + rx[0, i, :, cols].astype(F32)
+                + rx[1, i, :, cols].astype(F32) + rx[2, i, :, cols].astype(F32)
+            )
+            if j:
+                stage2[i].append(
+                    send(sx.at[i, yy], r2x.at[i, j - 1], SLOT["s2x"] + CH * j + i, to_y(j))
+                )
+                stage2[i][-1].start()
+
+    def reduce2(i):
+        take(*stage2[i])
+        upper = s2y[low_rows(i, x), :] + r2y[i, 0] + r2y[i, 1] + r2y[i, 2]
+        lower = sx[i, y] + r2x[i, 0] + r2x[i, 1] + r2x[i, 2]
+        for hh in range(2):
+            for l in range(4):
+                both = upper if l < 2 else lower
+                at = ZK * (l % 2)
+                t3[i, hh, l] = both[at : at + ZK, hh * PC : (hh + 1) * PC]
+        for at, dev in z_peers:
+            copy = send(
+                t3.at[i, lax.rem(h + at // 4, 2), ring4(zl, at % 4)], r3.at[i, at],
+                SLOT["s3"] + 8 * i + at, dev,
+            )
             copy.start()
-            stage2.append(copy)
-
-    for copy in lsends:
-        copy.wait_recv()
+            stage3[i].append(copy)
+
+    def reduce3(i):
+        take(*stage3[i])
+        piece = t3[i, h, zl]
+        for at in range(1, 8):
+            piece = piece + r3[i, at]
+        fin[i, x, zl] = piece.astype(BF16)
+        for d in (1, 3, 2):
+            agz[i].append(
+                send(fin.at[i, x, zl], fin.at[i, x, zl], SLOT["agz"] + 4 * i + d,
+                     {"dp_0": ring4(zl, d)})
+            )
+        go(*agz[i])
+
+    def gather(i):
+        take(*agz[i])
+        for d in (1, 3, 2):
+            agx[i].append(send(fin.at[i, x], fin.at[i, x], SLOT["agx"] + 4 * i + d, to_x(d)))
+        go(*agx[i])
+
+    reduce1(0)
+    reduce1(1)
+    reduce1(2)
+    take(*lsends)
     total = lsh[0]
     for i in range(1, 8):
         total = total + lsh[i]
     ldp[gid] = total
     lsends2 = [send(ldp.at[gid], ldp.at[gid], SLOT["ldp"] + at, dev) for at, dev in dp_peers]
-    for copy in lsends2:
-        copy.start()
-
-    for copy in stage2:
-        copy.wait_recv()
-    upper = s2y[pl.ds(pl.multiple_of(XK * x, 16), XK), :] + r2y[0] + r2y[1] + r2y[2]
-    lower = sx[y] + r2x[0] + r2x[1] + r2x[2]
-    for hh in range(2):
-        for l in range(4):
-            rows = upper if l < 2 else lower
-            t3[hh, l] = rows[24 * (l % 2) : 24 * (l % 2) + 24, hh * PC : (hh + 1) * PC]
-    stage3 = []
-    for at, dev in z_peers:
-        dh, dl = at // 4, at % 4
-        copy = send(
-            t3.at[lax.rem(h + dh, 2), ring4(zl, dl)], r3.at[at], SLOT["s3"] + at, dev
-        )
-        copy.start()
-        stage3.append(copy)
-    for copy in stage3:
-        copy.wait_recv()
-    piece = t3[h, zl]
-    for at in range(1, 8):
-        piece = piece + r3[at]
-    fin[x, zl] = piece.astype(BF16)
-
-    agz = [
-        send(fin.at[x, zl], fin.at[x, zl], SLOT["agz"] + d, {"dp_0": ring4(zl, d)})
-        for d in (1, 3, 2)
-    ]
-    for copy in agz:
-        copy.start()
-    for copy in agz:
-        copy.wait_recv()
-    agx = [send(fin.at[x], fin.at[x], SLOT["agx"] + d, to_x(d)) for d in (1, 3, 2)]
-    for copy in agx:
-        copy.start()
-
-    for copy in lsends2:
-        copy.wait_recv()
+    go(*lsends2)
+    reduce2(0)
+    reduce2(1)
+    reduce3(0)
+    reduce2(2)
+    gather(0)
+    reduce3(1)
+    gather(1)
+    reduce3(2)
+    take(*lsends2)
     total = ldp[0]
     for i in range(1, 16):
         total = total + ldp[i]
-    loss_o[...] = (total / (2.0 * KV * count))[0:1, 0:1]
-
-    for copy in agx:
-        copy.wait_recv()
-    ordered = []
-    for side in range(2):
-        for xx in range(4):
-            ordered += [fin[xx, 2 * side + l].astype(F32) for l in range(2)]
-    kt[...] = jnp.transpose(jnp.concatenate(ordered, axis=0))
+    loss_o[...] = (total / (2.0 * KV * count))[:, 0:1]
+    gather(2)
+    for i in range(CH):
+        take(*agx[i])
+    ordered = [
+        fin[i, xx, 2 * side + l].astype(F32)
+        for side in range(2) for i in range(CH) for xx in range(4) for l in range(2)
+    ]
+    kt[...] = jnp.transpose(jnp.concatenate(ordered, axis=0)).astype(BF16)
     osend = send(
         kt.at[pl.ds(pl.multiple_of((1 - c) * SL, 64), SL)], outs.at[:, my_cols],
         SLOT["out"], sib,
@@ -431,17 +472,18 @@
     osend.wait_recv()
     key_out = pltpu.make_async_copy(outs, key_o, lsem.at[4])
     key_out.start()
-    terms = outs[...] * w[...].astype(F32)
+    terms = outs[...].astype(F32) * w[...].astype(F32)
     summed = lax.dot_general(
         jnp.ones((8, KV), F32), terms, (((1,), (1,)), ((), ())),
         preferred_element_type=F32, precision=lax.Precision.HIGHEST,
     )
-    gain_o[...] = summed[0:1, :] / gain[...]
+    gain_o[...] = (summed[0:1, :] / own_gain).reshape(SL)
     key_out.wait()
 
     for copy in (
         [sib_w, sib_info, sib_tea, sib_hid, lsend, osend] + first + second + gsend + csend
-        + sum(handed.values(), []) + stage1 + lsends + stage2 + lsends2 + stage3 + agz + agx
+        + sum(handed.values(), []) + lsends + lsends2
+        + sum(stage1 + stage2 + stage3 + agz + agx, [])
     ):
         copy.wait_send()
 
@@ -453,23 +495,17 @@
 
 
 def body(hidden_in, teacher, norm_gain, w_key, group_rows, member):
-    core = lax.axis_index("shard_2")
-    gain = norm_gain.astype(F32)
-    row = lax.broadcasted_iota(jnp.int32, (8, PC), 0)
-    lane = lax.broadcasted_iota(jnp.int32, (8, PC), 1)
-    own = (row == 0) & (lane >= core * SL) & (lane < core * SL + SL)
-    live = (member[0, 0] * group_rows[0]).astype(F32)
-    info = jnp.where(own, jnp.concatenate([gain, gain])[None, :], jnp.where(row == 1, live, 0.0))
     vm = pl.BlockSpec(memory_space=pltpu.VMEM)
     hbm = pl.BlockSpec(memory_space=pl.ANY)
+    sm = pl.BlockSpec(memory_space=pltpu.SMEM)
     loss, grad_gain, grad_key = pl.pallas_call(
         kernel,
         out_shape=(
             jax.ShapeDtypeStruct((1, 1), F32),
-            jax.ShapeDtypeStruct((1, SL), F32),
-            jax.ShapeDtypeStruct((SL, KV), F32),
+            jax.ShapeDtypeStruct((SL,), F32),
+            jax.ShapeDtypeStruct((SL, KV), BF16),
         ),
-        in_specs=[hbm, vm, vm, vm, vm],
+        in_specs=[hbm, vm, vm, vm, sm, sm],
         out_specs=(vm, vm, hbm),
         scratch_shapes=[
             pltpu.VMEM((2, TOK, D), BF16),
@@ -479,25 +515,27 @@
             pltpu.VMEM((2, TOK, 128), F32),
             pltpu.VMEM((2 * TOK, HK), F32),
             pltpu.VMEM((HK, 2 * TOK), BF16),
-            pltpu.VMEM((4, HK, YB), BF16),
+            pltpu.VMEM((4, QK, YB), BF16),
+            pltpu.VMEM((QK, 4 * YB), BF16),
             pltpu.VMEM((3, QK, YB), BF16),
-            pltpu.VMEM((3, 4, XK, YB), BF16),
+            pltpu.VMEM((3, CH, XK, 4 * YB), BF16),
             pltpu.VMEM((QK, YB), F32),
-            pltpu.VMEM((4, XK, YB), F32),
-            pltpu.VMEM((3, XK, YB), F32),
-            pltpu.VMEM((3, XK, YB), F32),
-            pltpu.VMEM((2, 4, 24, PC), F32),
-            pltpu.VMEM((8, 24, PC), F32),
-            pltpu.VMEM((4, 4, 24, PC), BF16),
-            pltpu.VMEM((PC, HK), F32),
-            pltpu.VMEM((SL, KV), F32),
-            pltpu.VMEM((8, PC), F32),
-            pltpu.VMEM((8, 8, PC), F32),
-            pltpu.VMEM((16, 8, 128), F32),
-            pltpu.VMEM((8, 128), F32),
-            pltpu.VMEM((8, 128), F32),
-            pltpu.VMEM((8, 8, 128), F32),
-            pltpu.VMEM((16, 8, 128), F32),
+            pltpu.VMEM((CH, 4, XK, YB), F32),
+            pltpu.VMEM((CH, 3, XK, YB), F32),
+            pltpu.VMEM((CH, 3, XK, YB), F32),
+            pltpu.VMEM((CH, 2, 4, ZK, PC), F32),
+            pltpu.VMEM((CH, 8, ZK, PC), F32),
+            pltpu.VMEM((CH, 4, 4, ZK, PC), BF16),
+            pltpu.VMEM((PC, HK), BF16),
+            pltpu.VMEM((SL, KV), BF16),
+            pltpu.VMEM((1, PC + 128), F32),
+            pltpu.VMEM((1, PC + 128), F32),
+            pltpu.VMEM((8, 1, PC + 128), F32),
+            pltpu.VMEM((16, 1, 128), F32),
+            pltpu.VMEM((1, 128), F32),
+            pltpu.VMEM((1, 128), F32),
+            pltpu.VMEM((8, 1, 128), F32),
+            pltpu.VMEM((16, 1, 128), F32),
             pltpu.SemaphoreType.DMA((5,)),
             pltpu.SemaphoreType.DMA((N_SLOT,)),
             pltpu.SemaphoreType.DMA((N_SLOT,)),
@@ -506,8 +544,8 @@
         compiler_params=pltpu.CompilerParams(
             collective_id=0, has_side_effects=True, vmem_limit_bytes=62 * 2**20
         ),
-    )(hidden_in, teacher, w_key, gain[None, :], info)
-    return loss.reshape(()), grad_gain.reshape(SL), grad_key
+    )(hidden_in, teacher, w_key, norm_gain, group_rows, member)
+    return loss.reshape(()), grad_gain, grad_key.astype(F32)
 
 
 def solution(mesh):

time: 120 us -> 108 us (0.900)
  Pallas kernels: 110 us -> 101 us
  local copies, waits for them, and re-layouts: 3.45 us -> 1.25 us
    pallas_call x1, Pallas kernels: 110 us -> 101 us  [body(): pl.pallas_call(kernel, out_shape=(jax.ShapeDtypeStruct((1, 1), F32), jax....]
    convert_element_type x1, other arithmetic: 0.68 us -> 2.04 us  [body(): return (loss.reshape(()), grad_gain, grad_key.astype(F32))]
    pallas_call x1 -> x0, other arithmetic: 1.26 us -> none  [body(): pl.pallas_call(kernel, out_shape=(jax.ShapeDtypeStruct((1, 1), F32), jax....]
    broadcast_in_dim x1 -> x0, local copies, waits for them, and re-layouts: 1.24 us -> none  [body(): gain[None, :]]
where the time goes in v3:
time: 108 us
  Pallas kernels  101 us (94%)
  between operations  3.76 us (3%)
  other arithmetic  2.04 us (2%)
  local copies, waits for them, and re-layouts  1.25 us (1%)
    pallas_call x1, Pallas kernels, body(): pl.pallas_call(kernel, out_shape=(jax.ShapeDtypeStruct((1, 1), F32), jax....  101 us

profile of v3, /device:TPU:1, one launch (start us, length us, event | category | flops | bytes accessed | tf_op | source)
XLA Modules:
  0.0 107.8 jit_solution(17199255156425031913)
XLA Ops:
  1.9 100.8 %shard_map.85 = (f32[1,1]{1,0:T(1,128)}, f32[320]{0:T(512)}, bf16[320,768]{1,0:T(8,128)(2,1)}) custom-call(bf16[256,5120]{1,0:T(8,128)(2,1)} %hid.1, bf16[256,768]{1,0:T(8,128)(2,1)} %tea.1, bf16[320,768]{1,0:T(8,128)(2,1)} %w.1, bf16[320]{0:T(512)(128)(2,1)} %gain.1, s32[1]{0:T(128)S(6)} %copy.11.rows_of, s32[1,1]{1,0:T(1,128)S(6)} %copy.12.alive), custom_call_target="tpu_custom_call" | custom-call | tf_op jit(solution)/shard_map/pallas_call | solution.py:501
  102.7 2.0 %convert_element_type.3 = f32[320,768]{1,0:T(8,128)} convert(bf16[320,768]{1,0:T(8,128)(2,1)} %get-tuple-element.8) | non-fusion elementwise | flops 245760 | bytes 1474560 | tf_op jit(solution)/shard_map/convert_element_type | solution.py:548
  105.4 1.2 %copy.14 = f32[320]{0:T(512)} copy(f32[320]{0:T(512)} %get-tuple-element.13) | data formatting | bytes 2560

commit v4 on v3

v4 whole, which is shorter than its diff:
```python
import jax
import jax.numpy as jnp
from jax import lax
from jax.experimental import pallas as pl
from jax.experimental.pallas import tpu as pltpu
from jax.sharding import Mesh
from jax.sharding import PartitionSpec as P

SHARD = ("shard_0", "shard_1", "shard_2")
DP_SHARD = ("dp_0", "dp_1", "shard_0", "shard_1", "shard_2")
DP = ("dp_0", "dp_1")
MESH = pl.DeviceIdType.MESH
F32, BF16 = jnp.float32, jnp.bfloat16

EPSILON = 1e-06
SCALE = 1024.0

TOK = 256
D = 5120
KV = 768
HK = KV // 2
SL = 320
PC = 2 * SL
YB = 2 * PC
QK = HK // 2
CH = 3
CK = QK // CH
XK = CK // 4
ZK = XK // 2

HR = 80
DR = 2 * HR
SR = 80
SA = 48

def slots(*groups):
    place, at = {}, 0
    for name, count in groups:
        place[name] = at
        at += count
    return place, at


SLOT, N_SLOT = slots(
    *((name, 1) for name in ("info", "w", "tea", "hid", "lsib", "ginfo", "lsh", "cnt", "ldp")),
    ("wy", 12), ("wx", 8), ("wz", 3), ("qy", CH), ("qx", CH), ("ry", 2 * CH), ("rx", 2 * CH),
    ("s2y", CH), ("s2x", CH), ("s3", CH), ("agz", CH), ("agx", CH), ("out", CH),
)


def kernel(
    hid, tea, w, gain, rows_of, alive, loss_o, key_o,
    wv, hbuf, tbuf, wbuf, nbuf, inv, keys, dkt, gup, glow, qy, qx, ry, rx,
    s2y, sx, r2y, r2x, t3, r3, fin, kt, info, isib, gfull, cbuf, lown, lsib, lsh, ldp,
    lsem, ssem, rsem, zsem,
):
    zl, x = lax.axis_index("dp_0"), lax.axis_index("dp_1")
    h, y, c = (lax.axis_index(a) for a in SHARD)

    def ring4(v, d):
        return lax.rem(v + d, 4)

    def to_y(d):
        return {"shard_1": ring4(y, d)}

    def to_x(d):
        return {"dp_1": ring4(x, d)}

    sib = {"shard_2": 1 - c}

    def send(src, dst, slot, dev):
        return pltpu.make_async_remote_copy(
            src_ref=src, dst_ref=dst, send_sem=ssem.at[slot], recv_sem=rsem.at[slot],
            device_id=dev, device_id_type=MESH,
        )

    class Group:
        def __init__(self, slot, whole, parts):
            self.copies = [send(src, dst, slot, dev) for src, dst, dev in parts]
            self.whole = send(whole, whole, slot, sib)

        def start(self):
            for copy in self.copies:
                copy.start()

        def wait_recv(self):
            self.whole.wait_recv()

        def wait_send(self):
            self.whole.wait_send()

    shard_peers = [
        (dh * 4 + dy, {"shard_0": lax.rem(h + dh, 2), "shard_1": ring4(y, dy)})
        for dh in range(2) for dy in range(4) if dh or dy
    ]
    dp_peers = [
        (dl * 4 + dx, {"dp_0": ring4(zl, dl), "dp_1": ring4(x, dx)})
        for dl in range(4) for dx in range(4) if dl or dx
    ]
    z_peers = [
        (dh * 4 + dl, {"shard_0": lax.rem(h + dh, 2), "dp_0": ring4(zl, dl)})
        for dh in range(2) for dl in range(4) if dh or dl
    ]
    extra = [dev for at, dev in z_peers if at > 4]
    everyone = [sib] + [dev for _, dev in shard_peers + dp_peers] + extra

    own_rows = pl.ds(pl.multiple_of(h * PC + c * SL, 64), SL)
    my_cols = pl.ds(pl.multiple_of(c * HK, 128), HK)
    sib_cols = pl.ds(pl.multiple_of((1 - c) * HK, 128), HK)
    mine = y * 2 + h
    gid = zl * 4 + x

    own_hid = pltpu.make_async_copy(hid, hbuf.at[c], lsem.at[0])
    own_hid.start()
    own_w = pltpu.make_async_copy(w.at[:, my_cols], wbuf.at[y, own_rows], lsem.at[1])
    own_w.start()
    own_tea = pltpu.make_async_copy(tea.at[:, my_cols], tbuf.at[c], lsem.at[2])
    own_tea.start()
    stage_w = pltpu.make_async_copy(w, wv, lsem.at[3])
    stage_w.start()

    own_gain = gain[...].astype(F32).reshape(1, SL)
    lane = lax.broadcasted_iota(jnp.int32, (1, PC), 1)
    own = (lane >= c * SL) & (lane < c * SL + SL)
    info[:, 0:PC] = jnp.where(own, jnp.concatenate([own_gain, own_gain], axis=1), 0.0)
    live = (alive[...] * rows_of[...].reshape(1, 1)).astype(F32)
    info[:, PC:] = jnp.broadcast_to(live, (1, 128))

    barrier = pltpu.get_barrier_semaphore()
    for dev in everyone:
        pl.semaphore_signal(barrier, inc=1, device_id=dev, device_id_type=MESH)
    pl.semaphore_wait(barrier, len(everyone))

    stage_w.wait()
    sib_w = send(wv.at[:, sib_cols], wbuf.at[y, own_rows], SLOT["w"], sib)
    sib_w.start()
    sib_info = send(info, isib, SLOT["info"], sib)
    sib_info.start()
    sib_tea = send(tea.at[:, sib_cols], tbuf.at[c], SLOT["tea"], sib)
    sib_tea.start()
    sib_hid = send(hid, hbuf.at[c], SLOT["hid"], sib)
    sib_hid.start()

    edge = (zl == 0) | (zl == 3)
    over = {"shard_0": 1 - h, "dp_0": 3 - zl}
    inner = {"dp_0": jnp.where(zl == 0, 1, 2)}
    split = PC // 2 + SR * x

    def part(owner, half, at, n):
        return wbuf.at[owner, pl.ds(pl.multiple_of(half * PC + at, 16), n)]

    z_parts = ((split, SR), (0, DR), (DR, DR))

    def z_over(i):
        ref = part(y, h, *z_parts[i])
        return send(ref, ref, SLOT["wz"] + i, over)

    def z_in(i):
        ref = part(y, 1 - h, *z_parts[i])
        return pltpu.make_async_remote_copy(
            src_ref=ref, dst_ref=ref, send_sem=zsem.at[i], recv_sem=rsem.at[SLOT["wz"] + i],
            device_id=inner, device_id_type=MESH,
        )

    def z_relay(i):
        @pl.when(edge)
        def _():
            z_in(i).wait_recv()
            z_in(i).start()

    def z_take(i):
        @pl.when(jnp.logical_not(edge))
        def _():
            z_in(i).wait_recv()

    def y_copies(g):
        half = h if g == 0 else 1 - h
        back, ahead = ring4(y, 3), ring4(y, 1)
        plan = (
            (y, split, SR, 1), (y, split, SR, 3),
            (y, 0, DR, 1), (y, 0, DR, 3), (y, DR, DR, 1), (y, DR, DR, 3),
            (back, split, SA, 1), (ahead, split + SA, SR - SA, 3),
            (back, 0, HR, 1), (ahead, HR, HR, 3),
            (back, DR, HR, 1), (ahead, DR + HR, HR, 3),
        )
        groups = []
        for i in range(0, len(plan), 2):
            pair = [(part(owner, half, at, n), d) for owner, at, n, d in plan[i : i + 2]]
            total = sum(n for _, _, n, _ in plan[i : i + 2])
            groups.append(Group(
                SLOT["wy"] + 6 * g + i // 2, wbuf.at[0, pl.ds(0, total)],
                [(ref, ref, to_y(d)) for ref, d in pair],
            ))
        return groups

    first, second = y_copies(0), y_copies(1)
    handed = {}

    def hand(g, k):
        ref = part(ring4(y, k), h if g == 0 else 1 - h, split, SR)
        handed[g, k] = Group(
            SLOT["wx"] + 4 * g + k, wbuf.at[0, pl.ds(0, 3 * SR)],
            [(ref, ref, to_x(i)) for i in (1, 3, 2)],
        )
        handed[g, k].start()

    def take(*copies):
        for copy in copies:
            copy.wait_recv()

    def go(*copies):
        for copy in copies:
            copy.start()

    sib_info.wait_recv()
    gfull[mine] = info[...] + isib[...]
    gsend = Group(
        SLOT["ginfo"], gfull.at[pl.ds(0, 7)],
        [(gfull.at[mine], gfull.at[mine], dev) for _, dev in shard_peers],
    )
    gsend.start()
    own_w.wait()
    sib_w.wait_recv()
    go(first[0])

    @pl.when(edge)
    def _():
        z_over(0).start()

    go(first[1])

    @pl.when(edge)
    def _():
        z_over(1).start()
        z_over(2).start()

    def norms(which):
        @pl.loop(0, TOK // 32)
        def _(i):
            rows = pl.ds(pl.multiple_of(i * 32, 32), 32)
            v = hbuf[which, rows, :].astype(F32)
            mean = jnp.sum(v * v, axis=1, keepdims=True) * (1.0 / D)
            inv[which, rows, :] = jnp.broadcast_to(lax.rsqrt(mean + EPSILON), (32, 128))

    def normalize(yy, hh):
        src = (hh * 4 + yy) * PC
        dst = (yy * 2 + hh) * PC
        for which in range(2):
            @pl.loop(0, TOK // 64)
            def _(i):
                rows = pl.ds(pl.multiple_of(i * 64, 64), 64)
                out = pl.ds(pl.multiple_of(which * TOK + i * 64, 64), 64)
                scale = inv[which, rows, :]
                for lane in range(0, PC, 128):
                    by = gfull[yy * 2 + hh, :, lane : lane + 128]
                    v = hbuf[which, rows, src + lane : src + lane + 128].astype(F32)
                    nbuf[out, dst + lane : dst + lane + 128] = (v * scale * by).astype(BF16)

    def project(k, g, start=False):
        half = h if g == 0 else 1 - h
        owner = ring4(y, k)
        cols = pl.ds(pl.multiple_of(owner * YB + half * PC, 128), PC)
        rows = pl.ds(pl.multiple_of(half * PC, 64), PC)
        term = jnp.dot(nbuf[:, cols], wbuf[owner, rows, :], preferred_element_type=F32)
        keys[...] = term if start else keys[...] + term

    own_hid.wait()
    norms(c)
    take(first[0])
    go(first[3])
    hand(0, 3)
    hand(0, 1)
    go(first[2])
    z_relay(0)
    z_take(0)
    go(second[0])
    hand(1, 0)
    z_relay(1)
    take(gsend)
    group = gfull[0, :, PC:]
    for i in range(1, 8):
        group = group + gfull[i, :, PC:]
    cbuf[gid] = group
    csend = Group(
        SLOT["cnt"], cbuf.at[pl.ds(0, 15)],
        [(cbuf.at[gid], cbuf.at[gid], dev) for _, dev in dp_peers],
    )
    csend.start()
    sib_hid.wait_recv()
    norms(1 - c)
    z_relay(2)
    take(first[1])
    go(first[4])
    z_take(1)
    go(second[1])
    take(first[2])
    go(first[5])
    normalize(0, 0)
    take(second[0])
    go(second[3])
    hand(1, 3)
    hand(1, 1)
    normalize(0, 1)
    take(first[3])
    hand(0, 2)
    normalize(1, 0)
    z_take(2)
    go(second[2])
    normalize(1, 1)
    normalize(2, 0)
    take(second[1])
    go(second[4])
    take(second[3])
    hand(1, 2)
    normalize(2, 1)
    normalize(3, 0)
    normalize(3, 1)
    project(0, 0, True)
    take(second[2])
    go(second[5])
    take(handed[0, 3], handed[0, 1])
    project(3, 0)
    project(1, 0)
    take(handed[1, 0])
    project(0, 1)
    take(handed[0, 2], *first[4:])
    project(2, 0)
    take(csend)
    take(handed[1, 3], handed[1, 1])
    project(3, 1)
    project(1, 1)
    take(handed[1, 2], *second[4:])
    project(2, 1)

    count = cbuf[0]
    for i in range(1, 16):
        count = count + cbuf[i]
    count = count[:, 0:1]
    scale = SCALE / count
    sib_tea.wait_recv()
    own_tea.wait()
    own_n = info[:, PC : PC + 1]
    sib_n = isib[:, PC : PC + 1]
    position = lax.broadcasted_iota(jnp.int32, (TOK, 1), 0).astype(F32)
    squares = jnp.zeros((1, HK), F32)
    for which in range(2):
        live = jnp.where(c == which, own_n, sib_n)
        valid = jnp.where(position < live, 1.0, 0.0)
        rows = slice(which * TOK, (which + 1) * TOK)
        diff = keys[rows, :] - tbuf[which].astype(F32)
        squares = squares + jnp.sum(valid * diff * diff, axis=0, keepdims=True)
        dk = scale * valid * diff
        dkt[:, rows] = jnp.transpose(dk).astype(BF16)
    lown[...] = jnp.broadcast_to(jnp.sum(squares, axis=1, keepdims=True), (1, 128))
    lsend = send(lown, lsib, SLOT["lsib"], sib)
    lsend.start()

    def low_rows(i, xx):
        return pl.ds(pl.multiple_of(CK * i + XK * xx, 16), XK)

    def cols_of(j):
        return pl.ds(pl.multiple_of(ring4(y, j) * YB, 128), YB)

    relay = [[] for _ in range(CH)]
    stage1 = [[] for _ in range(CH)]
    for j in (2, 3, 1, 0):
        term = jnp.dot(dkt[...], nbuf[:, cols_of(j)], preferred_element_type=F32)
        gup[ring4(y, j)] = term[:QK].astype(BF16)
        glow[:, cols_of(j)] = term[QK:].astype(BF16)
        for i in range(CH):
            rows = pl.ds(CK * i, CK)
            if j == 2:
                relay[i].append(Group(
                    SLOT["qy"] + i, gup.at[0, rows],
                    [(gup.at[ring4(y, 2), rows, pl.ds(at * PC, PC)], qy.at[at, rows], to_y(d))
                     for at, d in enumerate((1, 3))],
                ))
                relay[i][0].start()
            at = 0 if j in (2, 1) else 1
            part_x = (
                glow.at[low_rows(i, ring4(x, 2)), cols_of(j)], qx.at[i, j], to_x(1 + 2 * at)
            )
            send(part_x[0], part_x[1], SLOT["qx"] + i, part_x[2]).start()
        for i in range(CH):
            rows = pl.ds(CK * i, CK)
            if j in (1, 3):
                at = 0 if j == 1 else 1
                lanes = pl.ds((1 - at) * PC, PC)
                send(
                    gup.at[ring4(y, j), rows, lanes], ry.at[at, rows, lanes],
                    SLOT["ry"] + i, to_y(j),
                ).start()
            at = 1 if j in (2, 1) else 0
            d = 1 + 2 * at
            send(
                glow.at[low_rows(i, ring4(x, d)), cols_of(j)], rx.at[at, i, :, cols_of(j)],
                SLOT["rx"] + i, to_x(d),
            ).start()
    for i in range(CH):
        rows = pl.ds(CK * i, CK)
        relay[i].append(Group(SLOT["qx"] + i, qx.at[i], []))
        stage1[i] += [
            Group(SLOT["ry"] + i, gup.at[0, rows], []),
            Group(SLOT["rx"] + i, rx.at[0, i], []),
        ]

    def combine(i):
        take(*relay[i])
        rows = slice(CK * i, CK * i + CK)
        late_y, late_x = [], []
        for at, d in enumerate((1, 3)):
            yy, lanes = ring4(y, d), slice(at * PC, (at + 1) * PC)
            both = gup[yy, rows, lanes].astype(F32) + qy[at, rows].astype(F32)
            gup[yy, rows, lanes] = both.astype(BF16)
            late_y.append((gup.at[yy, rows, lanes], ry.at[at, rows, lanes], to_y(d)))
        for at, d in enumerate((1, 3)):
            there = low_rows(i, ring4(x, d))
            for j in ((2, 1), (3, 0))[at]:
                both = glow[there, cols_of(j)].astype(F32) + qx[i, j].astype(F32)
                glow[there, cols_of(j)] = both.astype(BF16)
                late_x.append(
                    (glow.at[there, cols_of(j)], rx.at[at, i, :, cols_of(j)], to_x(d))
                )
        rows = pl.ds(CK * i, CK)
        stage1[i] += [
            Group(SLOT["ry"] + CH + i, gup.at[0, rows], late_y),
            Group(SLOT["rx"] + CH + i, rx.at[0, i], late_x),
        ]
        go(*stage1[i][2:])

    take(lsend)
    lsh[mine] = lown[...] + lsib[...]
    lsends = Group(
        SLOT["lsh"], lsh.at[pl.ds(0, 7)],
        [(lsh.at[mine], lsh.at[mine], dev) for _, dev in shard_peers],
    )
    lsends.start()

    stage2 = [[] for _ in range(CH)]
    stage3 = [[] for _ in range(CH)]
    agz = [[] for _ in range(CH)]
    agx = [[] for _ in range(CH)]

    def reduce1(i):
        take(*stage1[i])
        rows = slice(CK * i, CK * i + CK)
        s2y[rows] = (
            gup[y, rows].astype(F32) + ry[0, rows].astype(F32) + ry[1, rows].astype(F32)
        )
        stage2[i].append(Group(
            SLOT["s2y"] + i, r2y.at[i],
            [(s2y.at[low_rows(i, ring4(x, d))], r2y.at[i, d - 1], to_x(d)) for d in (1, 3, 2)],
        ))
        stage2[i][0].start()
        for j in (1, 3, 2, 0):
            yy = ring4(y, j)
            cols = pl.ds(pl.multiple_of(yy * YB, 128), YB)
            sx[i, yy] = (
                glow[low_rows(i, x), cols].astype(F32) + rx[0, i, :, cols].astype(F32)
                + rx[1, i, :, cols].astype(F32)
            )
            if j:
                send(sx.at[i, yy], r2x.at[i, j - 1], SLOT["s2x"] + i, to_y(j)).start()
        stage2[i].append(Group(SLOT["s2x"] + i, r2x.at[i], []))

    def reduce2(i):
        take(*stage2[i])
        upper = s2y[low_rows(i, x), :] + r2y[i, 0] + r2y[i, 1] + r2y[i, 2]
        lower = sx[i, y] + r2x[i, 0] + r2x[i, 1] + r2x[i, 2]
        for hh in range(2):
            for l in range(4):
                both = upper if l < 2 else lower
                at = ZK * (l % 2)
                t3[i, hh, l] = both[at : at + ZK, hh * PC : (hh + 1) * PC]
        stage3[i].append(Group(
            SLOT["s3"] + i, r3.at[i, pl.ds(1, 7)],
            [(t3.at[i, lax.rem(h + at // 4, 2), ring4(zl, at % 4)], r3.at[i, at], dev)
             for at, dev in z_peers],
        ))
        stage3[i][0].start()

    def reduce3(i):
        take(*stage3[i])
        piece = t3[i, h, zl]
        for at in range(1, 8):
            piece = piece + r3[i, at]
        fin[c, i, x, zl] = piece.astype(BF16)
        agz[i].append(Group(
            SLOT["agz"] + i, fin.at[c, i, x, pl.ds(0, 3)],
            [(fin.at[c, i, x, zl], fin.at[c, i, x, zl], {"dp_0": ring4(zl, d)})
             for d in (1, 3, 2)],
        ))
        agz[i][0].start()

    def gather(i):
        take(*agz[i])
        agx[i].append(Group(
            SLOT["agx"] + i, fin.at[c, i, pl.ds(0, 3)],
            [(fin.at[c, i, x], fin.at[c, i, x], to_x(d)) for d in (1, 3, 2)],
        ))
        agx[i][0].start()

    def share(i):
        take(*agx[i])
        osend.append(send(fin.at[c, i], fin.at[c, i], SLOT["out"] + i, sib))
        osend[i].start()

    def drain(copies):
        for copy in copies:
            copy.wait_send()

    osend = []
    combine(0)
    combine(1)
    combine(2)
    drain([sib_w, sib_info, sib_tea, sib_hid, gsend, csend] + first + second)
    drain(handed.values())

    @pl.when(edge)
    def _():
        for i in range(3):
            z_over(i).wait_send()
            z_in(i).wait_send()

    reduce1(0)
    reduce1(1)
    reduce1(2)
    drain([lsend] + sum(relay + stage1, []))
    take(lsends)
    total = lsh[0]
    for i in range(1, 8):
        total = total + lsh[i]
    ldp[gid] = total
    lsends2 = Group(
        SLOT["ldp"], ldp.at[pl.ds(0, 15)],
        [(ldp.at[gid], ldp.at[gid], dev) for _, dev in dp_peers],
    )
    lsends2.start()
    reduce2(0)
    reduce2(1)
    reduce3(0)
    reduce2(2)
    reduce3(1)
    drain([lsends] + sum(stage2, []))
    gather(0)
    reduce3(2)
    gather(1)
    take(lsends2)
    total = ldp[0]
    for i in range(1, 16):
        total = total + ldp[i]
    loss_o[...] = (total / (2.0 * KV * count))[:, 0:1]
    share(0)
    gather(2)
    share(1)
    drain([lsends2] + sum(stage3 + agz, []) + agx[0] + agx[1])
    share(2)
    take(*osend)
    ordered = [
        fin[half, i, xx, 2 * side + l].astype(F32)
        for half in range(2) for side in range(2) for i in range(CH)
        for xx in range(4) for l in range(2)
    ]
    kt[...] = jnp.transpose(jnp.concatenate(ordered, axis=0)).astype(BF16)
    key_out = pltpu.make_async_copy(
        kt.at[pl.ds(pl.multiple_of(c * SL, 64), SL)], key_o, lsem.at[4]
    )
    key_out.start()
    drain(agx[2] + osend)
    key_out.wait()


def finish(key, w, gain, loss, loss_o, gain_o, key_o):
    grad = key[...].astype(F32)
    key_o[...] = grad
    loss_o[...] = loss[...]
    summed = lax.dot_general(
        jnp.ones((8, KV), F32), grad * w[...].astype(F32), (((1,), (1,)), ((), ())),
        preferred_element_type=F32, precision=lax.Precision.HIGHEST,
    )
    gain_o[...] = (summed[0:1, :] / gain[...].astype(F32).reshape(1, SL)).reshape(SL)


def body(hidden_in, teacher, norm_gain, w_key, group_rows, member):
    vm = pl.BlockSpec(memory_space=pltpu.VMEM)
    hbm = pl.BlockSpec(memory_space=pl.ANY)
    loss, key = pl.pallas_call(
        kernel,
        out_shape=(
            jax.ShapeDtypeStruct((1, 1), F32),
            jax.ShapeDtypeStruct((SL, KV), BF16),
        ),
        in_specs=[hbm, hbm, hbm, vm, vm, vm],
        out_specs=(vm, hbm),
        scratch_shapes=[
            pltpu.VMEM((SL, KV), BF16),
            pltpu.VMEM((2, TOK, D), BF16),
            pltpu.VMEM((2, TOK, HK), BF16),
            pltpu.VMEM((4, YB, HK), BF16),
            pltpu.VMEM((2 * TOK, D), BF16),
            pltpu.VMEM((2, TOK, 128), F32),
            pltpu.VMEM((2 * TOK, HK), F32),
            pltpu.VMEM((HK, 2 * TOK), BF16),
            pltpu.VMEM((4, QK, YB), BF16),
            pltpu.VMEM((QK, 4 * YB), BF16),
            pltpu.VMEM((2, QK, PC), BF16),
            pltpu.VMEM((CH, 4, XK, YB), BF16),
            pltpu.VMEM((2, QK, YB), BF16),
            pltpu.VMEM((2, CH, XK, 4 * YB), BF16),
            pltpu.VMEM((QK, YB), F32),
            pltpu.VMEM((CH, 4, XK, YB), F32),
            pltpu.VMEM((CH, 3, XK, YB), F32),
            pltpu.VMEM((CH, 3, XK, YB), F32),
            pltpu.VMEM((CH, 2, 4, ZK, PC), F32),
            pltpu.VMEM((CH, 8, ZK, PC), F32),
            pltpu.VMEM((2, CH, 4, 4, ZK, PC), BF16),
            pltpu.VMEM((PC, KV), BF16),
            pltpu.VMEM((1, PC + 128), F32),
            pltpu.VMEM((1, PC + 128), F32),
            pltpu.VMEM((8, 1, PC + 128), F32),
            pltpu.VMEM((16, 1, 128), F32),
            pltpu.VMEM((1, 128), F32),
            pltpu.VMEM((1, 128), F32),
            pltpu.VMEM((8, 1, 128), F32),
            pltpu.VMEM((16, 1, 128), F32),
            pltpu.SemaphoreType.DMA((5,)),
            pltpu.SemaphoreType.DMA((N_SLOT,)),
            pltpu.SemaphoreType.DMA((N_SLOT,)),
            pltpu.SemaphoreType.DMA((3,)),
        ],
        compiler_params=pltpu.CompilerParams(
            collective_id=0, has_side_effects=True, vmem_limit_bytes=62 * 2**20
        ),
    )(hidden_in, teacher, w_key, norm_gain, group_rows, member)
    loss, grad_gain, grad_key = pl.pallas_call(
        finish,
        out_shape=(
            jax.ShapeDtypeStruct((1, 1), F32),
            jax.ShapeDtypeStruct((SL,), F32),
            jax.ShapeDtypeStruct((SL, KV), F32),
        ),
        in_specs=[vm] * 4,
        out_specs=(vm, vm, vm),
    )(key, w_key, norm_gain, loss)
    return loss.reshape(()), grad_gain, grad_key


def solution(mesh):
    split = Mesh(mesh.devices.reshape(4, 4, 2, 4, 2), DP_SHARD)
    return jax.shard_map(
        body,
        mesh=split,
        in_specs=(
            P(DP_SHARD, None),
            P(DP_SHARD, None),
            P(SHARD),
            P(SHARD, None),
            P(DP),
            P(DP, SHARD),
        ),
        out_specs=(P(), P(SHARD), P(SHARD, None)),
        check_vma=False,
    )
```

time: 108 us -> 98.9 us (0.916)
  Pallas kernels: 101 us -> 96.8 us
  other arithmetic: 2.04 us -> 0 us
  between operations: 3.76 us -> 1.93 us
  local copies, waits for them, and re-layouts: 1.25 us -> 0 us
    pallas_call x1, Pallas kernels: 101 us -> 93 us  [body(): pl.pallas_call(kernel, out_shape=(jax.ShapeDtypeStruct((1, 1), F32), jax....]
    pallas_call x0 -> x1, Pallas kernels: none -> 3.76 us  [body(): pl.pallas_call(finish, out_shape=(jax.ShapeDtypeStruct((1, 1), F32), jax....]
    convert_element_type x1 -> x0, other arithmetic: 2.04 us -> none  [body(): return (loss.reshape(()), grad_gain, grad_key.astype(F32))]
    unnamed x1 -> x0, local copies, waits for them, and re-layouts: 1.25 us -> none
where the time goes in v4:
time: 98.9 us; the launch traced here: 98.7 us
  Pallas kernels  96.8 us (98%)
  between operations  1.93 us (2%)
    pallas_call x1, Pallas kernels, body(): pl.pallas_call(kernel, out_shape=(jax.ShapeDtypeStruct((1, 1), F32), jax....  93 us
    pallas_call x1, Pallas kernels, body(): pl.pallas_call(finish, out_shape=(jax.ShapeDtypeStruct((1, 1), F32), jax....  3.76 us

profile of v4, /device:TPU:1, one launch (start us, length us, event | category | flops | bytes accessed | tf_op | source)
XLA Modules:
  0.0 98.7 jit_solution(12797696879657875042)
XLA Ops:
  1.9 93.0 %shard_map.85 = (f32[1,1]{1,0:T(1,128)}, bf16[320,768]{1,0:T(8,128)(2,1)}) custom-call(bf16[256,5120]{1,0:T(8,128)(2,1)} %hid.1, bf16[256,768]{1,0:T(8,128)(2,1)} %tea.1, bf16[320,768]{1,0:T(8,128)(2,1)} %w.3, bf16[320]{0:T(512)(128)(2,1)} %gain.3, s32[1]{0:T(128)S(6)} %copy.9.rows_of, s32[1,1]{1,0:T(1,128)S(6)} %copy.10.alive), custom_call_target="tpu_custom_call" | custom-call | tf_op jit(solution)/shard_map/pallas_call | solution.py:587
  95.0 3.8 %shard_map.86 = (f32[1,1]{1,0:T(1,128)}, f32[320]{0:T(512)}, f32[320,768]{1,0:T(8,128)}) custom-call(bf16[320,768]{1,0:T(8,128)(2,1)} %get-tuple-element.8.key, bf16[320,768]{1,0:T(8,128)(2,1)} %w.3, bf16[320]{0:T(512)(128)(2,1)} %gain.3, f32[1,1]{1,0:T(1,128)} %get-tuple-element.9.loss), custom_call_target="tpu_custom_call" | custom-call | tf_op jit(solution)/shard_map/pallas_call | solution.py:635

commit v5 on v4

--- a/solution.py
+++ b/solution.py
@@ -49,9 +49,9 @@
 
 
 def kernel(
-    hid, tea, w, gain, rows_of, alive, loss_o, key_o,
+    hid, tea, w, gain, rows_of, alive, loss_o, gain_o, key_o,
     wv, hbuf, tbuf, wbuf, nbuf, inv, keys, dkt, gup, glow, qy, qx, ry, rx,
-    s2y, sx, r2y, r2x, t3, r3, fin, kt, info, isib, gfull, cbuf, lown, lsib, lsh, ldp,
+    s2y, s2b, sx, sb, r2y, r2x, t3, t3b, r3, pown, prol, psib, fin, kt, info, isib, gfull, cbuf, lown, lsib, lsh, ldp,
     lsem, ssem, rsem, zsem,
 ):
     zl, x = lax.axis_index("dp_0"), lax.axis_index("dp_1")
@@ -444,37 +444,46 @@
     def reduce1(i):
         take(*stage1[i])
         rows = slice(CK * i, CK * i + CK)
-        s2y[rows] = (
+        total = (
             gup[y, rows].astype(F32) + ry[0, rows].astype(F32) + ry[1, rows].astype(F32)
         )
+        s2y[rows] = total
+        s2b[rows] = total.astype(BF16)
         stage2[i].append(Group(
             SLOT["s2y"] + i, r2y.at[i],
-            [(s2y.at[low_rows(i, ring4(x, d))], r2y.at[i, d - 1], to_x(d)) for d in (1, 3, 2)],
+            [(s2b.at[low_rows(i, ring4(x, d))], r2y.at[i, d - 1], to_x(d)) for d in (1, 3, 2)],
         ))
         stage2[i][0].start()
         for j in (1, 3, 2, 0):
-            yy = ring4(y, j)
-            cols = pl.ds(pl.multiple_of(yy * YB, 128), YB)
-            sx[i, yy] = (
+            cols = cols_of(j)
+            total = (
                 glow[low_rows(i, x), cols].astype(F32) + rx[0, i, :, cols].astype(F32)
                 + rx[1, i, :, cols].astype(F32)
             )
             if j:
-                send(sx.at[i, yy], r2x.at[i, j - 1], SLOT["s2x"] + i, to_y(j)).start()
+                sb[i, j - 1] = total.astype(BF16)
+                send(sb.at[i, j - 1], r2x.at[i, j - 1], SLOT["s2x"] + i, to_y(j)).start()
+            else:
+                sx[i] = total
         stage2[i].append(Group(SLOT["s2x"] + i, r2x.at[i], []))
 
     def reduce2(i):
         take(*stage2[i])
-        upper = s2y[low_rows(i, x), :] + r2y[i, 0] + r2y[i, 1] + r2y[i, 2]
-        lower = sx[i, y] + r2x[i, 0] + r2x[i, 1] + r2x[i, 2]
+        upper = s2y[low_rows(i, x), :]
+        lower = sx[i]
+        for d in range(3):
+            upper = upper + r2y[i, d].astype(F32)
+            lower = lower + r2x[i, d].astype(F32)
         for hh in range(2):
             for l in range(4):
                 both = upper if l < 2 else lower
                 at = ZK * (l % 2)
-                t3[i, hh, l] = both[at : at + ZK, hh * PC : (hh + 1) * PC]
+                block = both[at : at + ZK, hh * PC : (hh + 1) * PC]
+                t3[i, hh, l] = block
+                t3b[i, hh, l] = block.astype(BF16)
         stage3[i].append(Group(
             SLOT["s3"] + i, r3.at[i, pl.ds(1, 7)],
-            [(t3.at[i, lax.rem(h + at // 4, 2), ring4(zl, at % 4)], r3.at[i, at], dev)
+            [(t3b.at[i, lax.rem(h + at // 4, 2), ring4(zl, at % 4)], r3.at[i, at], dev)
              for at, dev in z_peers],
         ))
         stage3[i][0].start()
@@ -483,33 +492,34 @@
         take(*stage3[i])
         piece = t3[i, h, zl]
         for at in range(1, 8):
-            piece = piece + r3[i, at]
-        fin[c, i, x, zl] = piece.astype(BF16)
+            piece = piece + r3[i, at].astype(F32)
+        pown[i] = piece
+        prol[i] = jnp.concatenate([piece[:, SL:], piece[:, :SL]], axis=1)
+        swaps.append(send(prol.at[i], psib.at[i], SLOT["out"] + i, sib))
+        swaps[i].start()
+
+    def scatter(i):
+        take(swaps[i])
+        fin[i, x, zl] = jnp.where(own, pown[i], psib[i])
         agz[i].append(Group(
-            SLOT["agz"] + i, fin.at[c, i, x, pl.ds(0, 3)],
-            [(fin.at[c, i, x, zl], fin.at[c, i, x, zl], {"dp_0": ring4(zl, d)})
-             for d in (1, 3, 2)],
+            SLOT["agz"] + i, fin.at[i, x, pl.ds(0, 3)],
+            [(fin.at[i, x, zl], fin.at[i, x, zl], {"dp_0": ring4(zl, d)}) for d in (1, 3, 2)],
         ))
         agz[i][0].start()
 
     def gather(i):
         take(*agz[i])
         agx[i].append(Group(
-            SLOT["agx"] + i, fin.at[c, i, pl.ds(0, 3)],
-            [(fin.at[c, i, x], fin.at[c, i, x], to_x(d)) for d in (1, 3, 2)],
+            SLOT["agx"] + i, fin.at[i, pl.ds(0, 3)],
+            [(fin.at[i, x], fin.at[i, x], to_x(d)) for d in (1, 3, 2)],
         ))
         agx[i][0].start()
-
-    def share(i):
-        take(*agx[i])
-        osend.append(send(fin.at[c, i], fin.at[c, i], SLOT["out"] + i, sib))
-        osend[i].start()
 
     def drain(copies):
         for copy in copies:
             copy.wait_send()
 
-    osend = []
+    swaps = []
     combine(0)
     combine(1)
     combine(2)
@@ -540,58 +550,70 @@
     reduce2(1)
     reduce3(0)
     reduce2(2)
+    scatter(0)
     reduce3(1)
     drain([lsends] + sum(stage2, []))
+    scatter(1)
     gather(0)
     reduce3(2)
+    scatter(2)
     gather(1)
     take(lsends2)
     total = ldp[0]
     for i in range(1, 16):
         total = total + ldp[i]
     loss_o[...] = (total / (2.0 * KV * count))[:, 0:1]
-    share(0)
+    drain([lsends2] + sum(stage3, []) + swaps)
     gather(2)
-    share(1)
-    drain([lsends2] + sum(stage3 + agz, []) + agx[0] + agx[1])
-    share(2)
-    take(*osend)
+    drain(agz[0] + agz[1] + agx[0])
+    for i in range(CH):
+        take(*agx[i])
     ordered = [
-        fin[half, i, xx, 2 * side + l].astype(F32)
-        for half in range(2) for side in range(2) for i in range(CH)
-        for xx in range(4) for l in range(2)
+        fin[i, xx, 2 * side + l]
+        for side in range(2) for i in range(CH) for xx in range(4) for l in range(2)
     ]
-    kt[...] = jnp.transpose(jnp.concatenate(ordered, axis=0)).astype(BF16)
-    key_out = pltpu.make_async_copy(
-        kt.at[pl.ds(pl.multiple_of(c * SL, 64), SL)], key_o, lsem.at[4]
+    kt[...] = jnp.transpose(jnp.concatenate(ordered, axis=0))
+    outs = [
+        pltpu.make_async_copy(
+            kt.at[pl.ds(half * SL, SL)], key_o.at[:, pl.ds(half * HK, HK)], lsem.at[4 + half]
+        )
+        for half in range(2)
+    ]
+    go(*outs)
+    terms = (
+        kt[:SL, :] * wv[:, :HK].astype(F32) + kt[SL:, :] * wv[:, HK:].astype(F32)
     )
-    key_out.start()
-    drain(agx[2] + osend)
-    key_out.wait()
-
-
-def finish(key, w, gain, loss, loss_o, gain_o, key_o):
-    grad = key[...].astype(F32)
-    key_o[...] = grad
-    loss_o[...] = loss[...]
     summed = lax.dot_general(
-        jnp.ones((8, KV), F32), grad * w[...].astype(F32), (((1,), (1,)), ((), ())),
+        jnp.ones((8, HK), F32), terms, (((1,), (1,)), ((), ())),
         preferred_element_type=F32, precision=lax.Precision.HIGHEST,
     )
-    gain_o[...] = (summed[0:1, :] / gain[...].astype(F32).reshape(1, SL)).reshape(SL)
+    gain_o[...] = summed[0:1, :] / own_gain
+    drain(agz[2] + agx[1] + agx[2])
+    for copy in outs:
+        copy.wait()
+
+
+def finish(key, gain, loss, loss_o, gain_o, key_o):
+    key_o[...] = key[...]
+
+    @pl.when(pl.program_id(0) == 0)
+    def _():
+        loss_o[...] = loss[...]
+        gain_o[...] = gain[...].reshape(SL)
 
 
 def body(hidden_in, teacher, norm_gain, w_key, group_rows, member):
     vm = pl.BlockSpec(memory_space=pltpu.VMEM)
     hbm = pl.BlockSpec(memory_space=pl.ANY)
-    loss, key = pl.pallas_call(
+    loss, gain, key = pl.pallas_call(
         kernel,
         out_shape=(
             jax.ShapeDtypeStruct((1, 1), F32),
-            jax.ShapeDtypeStruct((SL, KV), BF16),
+            jax.ShapeDtypeStruct((1, SL), F32),
+            jax.ShapeDtypeStruct((SL, KV), F32),
         ),
         in_specs=[hbm, hbm, hbm, vm, vm, vm],
-        out_specs=(vm, hbm),
+        out_specs=(vm, vm, hbm),
         scratch_shapes=[
             pltpu.VMEM((SL, KV), BF16),
             pltpu.VMEM((2, TOK, D), BF16),
@@ -608,13 +630,19 @@
             pltpu.VMEM((2, QK, YB), BF16),
             pltpu.VMEM((2, CH, XK, 4 * YB), BF16),
             pltpu.VMEM((QK, YB), F32),
-            pltpu.VMEM((CH, 4, XK, YB), F32),
-            pltpu.VMEM((CH, 3, XK, YB), F32),
-            pltpu.VMEM((CH, 3, XK, YB), F32),
+            pltpu.VMEM((QK, YB), BF16),
+            pltpu.VMEM((CH, XK, YB), F32),
+            pltpu.VMEM((CH, 3, XK, YB), BF16),
+            pltpu.VMEM((CH, 3, XK, YB), BF16),
+            pltpu.VMEM((CH, 3, XK, YB), BF16),
             pltpu.VMEM((CH, 2, 4, ZK, PC), F32),
-            pltpu.VMEM((CH, 8, ZK, PC), F32),
-            pltpu.VMEM((2, CH, 4, 4, ZK, PC), BF16),
-            pltpu.VMEM((PC, KV), BF16),
+            pltpu.VMEM((CH, 2, 4, ZK, PC), BF16),
+            pltpu.VMEM((CH, 8, ZK, PC), BF16),
+            pltpu.VMEM((CH, ZK, PC), F32),
+            pltpu.VMEM((CH, ZK, PC), F32),
+            pltpu.VMEM((CH, ZK, PC), F32),
+            pltpu.VMEM((CH, 4, 4, ZK, PC), F32),
+            pltpu.VMEM((PC, HK), F32),
             pltpu.VMEM((1, PC + 128), F32),
             pltpu.VMEM((1, PC + 128), F32),
             pltpu.VMEM((8, 1, PC + 128), F32),
@@ -623,7 +651,7 @@
             pltpu.VMEM((1, 128), F32),
             pltpu.VMEM((8, 1, 128), F32),
             pltpu.VMEM((16, 1, 128), F32),
-            pltpu.SemaphoreType.DMA((5,)),
+            pltpu.SemaphoreType.DMA((6,)),
             pltpu.SemaphoreType.DMA((N_SLOT,)),
             pltpu.SemaphoreType.DMA((N_SLOT,)),
             pltpu.SemaphoreType.DMA((3,)),
@@ -639,9 +667,18 @@
             jax.ShapeDtypeStruct((SL,), F32),
             jax.ShapeDtypeStruct((SL, KV), F32),
         ),
-        in_specs=[vm] * 4,
-        out_specs=(vm, vm, vm),
-    )(key, w_key, norm_gain, loss)
+        grid=(4,),
+        in_specs=[
+            pl.BlockSpec((SL // 4, KV), lambda i: (i, 0)),
+            pl.BlockSpec((1, SL), lambda i: (0, 0)),
+            pl.BlockSpec((1, 1), lambda i: (0, 0)),
+        ],
+        out_specs=(
+            pl.BlockSpec((1, 1), lambda i: (0, 0)),
+            pl.BlockSpec((SL,), lambda i: (0,)),
+            pl.BlockSpec((SL // 4, KV), lambda i: (i, 0)),
+        ),
+    )(key, gain, loss)
     return loss.reshape(()), grad_gain, grad_key
 
 

time: 98.9 us -> 96.2 us (0.973)
  Pallas kernels: 96.8 us -> 94.1 us
    pallas_call x1, Pallas kernels: 93 us -> 90 us  [body(): pl.pallas_call(kernel, out_shape=(jax.ShapeDtypeStruct((1, 1), F32), jax....]
where the time goes in v5:
time: 96.2 us; the launch traced here: 96 us
  Pallas kernels  94.1 us (98%)
  between operations  1.93 us (2%)
    pallas_call x1, Pallas kernels, body(): pl.pallas_call(kernel, out_shape=(jax.ShapeDtypeStruct((1, 1), F32), jax....  90 us
    pallas_call x1, Pallas kernels, body(): pl.pallas_call(finish, out_shape=(jax.ShapeDtypeStruct((1, 1), F32), jax....  4.05 us

profile of v5, /device:TPU:1, one launch (start us, length us, event | category | flops | bytes accessed | tf_op | source)
XLA Modules:
  0.0 96.0 jit_solution(2769877658617809900)
XLA Ops:
  1.9 90.0 %shard_map.85 = (f32[1,1]{1,0:T(1,128)}, f32[1,320]{1,0:T(1,128)}, f32[320,768]{1,0:T(8,128)}) custom-call(bf16[256,5120]{1,0:T(8,128)(2,1)} %hid.1, bf16[256,768]{1,0:T(8,128)(2,1)} %tea.1, bf16[320,768]{1,0:T(8,128)(2,1)} %w.1, bf16[320]{0:T(512)(128)(2,1)} %gain.1, s32[1]{0:T(128)S(6)} %copy.9.rows_of, s32[1,1]{1,0:T(1,128)S(6)} %copy.10.alive), custom_call_target="tpu_custom_call" | custom-call | tf_op jit(solution)/shard_map/pallas_call | solution.py:608
  92.0 4.0 %shard_map.86 = (f32[1,1]{1,0:T(1,128)}, f32[320]{0:T(512)}, f32[320,768]{1,0:T(8,128)}) custom-call(f32[320,768]{1,0:T(8,128)} %get-tuple-element.9.key, f32[1,320]{1,0:T(1,128)} %get-tuple-element.10.gain, f32[1,1]{1,0:T(1,128)} %get-tuple-element.11.loss), custom_call_target="tpu_custom_call" | custom-call | tf_op jit(solution)/shard_map/pallas_call | solution.py:663

commit v6 on v5

--- a/solution.py
+++ b/solution.py
@@ -44,7 +44,7 @@
 SLOT, N_SLOT = slots(
     *((name, 1) for name in ("info", "w", "tea", "hid", "lsib", "ginfo", "lsh", "cnt", "ldp")),
     ("wy", 12), ("wx", 8), ("wz", 3), ("qy", CH), ("qx", CH), ("ry", 2 * CH), ("rx", 2 * CH),
-    ("s2y", CH), ("s2x", CH), ("s3", CH), ("agz", CH), ("agx", CH), ("out", CH),
+    ("s2y", CH), ("s2x", CH), ("s3", CH), ("agz", CH), ("agx", CH), ("agf", CH), ("out", CH),
 )
 
 
@@ -110,14 +110,18 @@
     mine = y * 2 + h
     gid = zl * 4 + x
 
+    stage_w = pltpu.make_async_copy(w, wv, lsem.at[3])
+    stage_w.start()
+    barrier = pltpu.get_barrier_semaphore()
+    for dev in everyone:
+        pl.semaphore_signal(barrier, inc=1, device_id=dev, device_id_type=MESH)
+
     own_hid = pltpu.make_async_copy(hid, hbuf.at[c], lsem.at[0])
     own_hid.start()
     own_w = pltpu.make_async_copy(w.at[:, my_cols], wbuf.at[y, own_rows], lsem.at[1])
     own_w.start()
     own_tea = pltpu.make_async_copy(tea.at[:, my_cols], tbuf.at[c], lsem.at[2])
     own_tea.start()
-    stage_w = pltpu.make_async_copy(w, wv, lsem.at[3])
-    stage_w.start()
 
     own_gain = gain[...].astype(F32).reshape(1, SL)
     lane = lax.broadcasted_iota(jnp.int32, (1, PC), 1)
@@ -126,9 +130,6 @@
     live = (alive[...] * rows_of[...].reshape(1, 1)).astype(F32)
     info[:, PC:] = jnp.broadcast_to(live, (1, 128))
 
-    barrier = pltpu.get_barrier_semaphore()
-    for dev in everyone:
-        pl.semaphore_signal(barrier, inc=1, device_id=dev, device_id_type=MESH)
     pl.semaphore_wait(barrier, len(everyone))
 
     stage_w.wait()
@@ -342,19 +343,14 @@
     own_n = info[:, PC : PC + 1]
     sib_n = isib[:, PC : PC + 1]
     position = lax.broadcasted_iota(jnp.int32, (TOK, 1), 0).astype(F32)
-    squares = jnp.zeros((1, HK), F32)
     for which in range(2):
         live = jnp.where(c == which, own_n, sib_n)
         valid = jnp.where(position < live, 1.0, 0.0)
         rows = slice(which * TOK, (which + 1) * TOK)
         diff = keys[rows, :] - tbuf[which].astype(F32)
-        squares = squares + jnp.sum(valid * diff * diff, axis=0, keepdims=True)
+        keys[rows, :] = valid * diff
         dk = scale * valid * diff
         dkt[:, rows] = jnp.transpose(dk).astype(BF16)
-    lown[...] = jnp.broadcast_to(jnp.sum(squares, axis=1, keepdims=True), (1, 128))
-    lsend = send(lown, lsib, SLOT["lsib"], sib)
-    lsend.start()
-
     def low_rows(i, xx):
         return pl.ds(pl.multiple_of(CK * i + XK * xx, 16), XK)
 
@@ -363,48 +359,43 @@
 
     relay = [[] for _ in range(CH)]
     stage1 = [[] for _ in range(CH)]
-    for j in (2, 3, 1, 0):
+    def issue(i, j):
+        rows = pl.ds(CK * i, CK)
+        if j == 2:
+            relay[i].append(Group(
+                SLOT["qy"] + i, gup.at[0, rows],
+                [(gup.at[ring4(y, 2), rows, pl.ds(at * PC, PC)], qy.at[at, rows], to_y(d))
+                 for at, d in enumerate((1, 3))],
+            ))
+            relay[i][0].start()
+        via, past = (1, 3) if j in (2, 1) else (3, 1)
+        send(
+            glow.at[low_rows(i, ring4(x, 2)), cols_of(j)], qx.at[i, j],
+            SLOT["qx"] + i, to_x(via),
+        ).start()
+        if j in (1, 3):
+            at = 0 if j == 1 else 1
+            lanes = pl.ds((1 - at) * PC, PC)
+            send(
+                gup.at[ring4(y, j), rows, lanes], ry.at[at, rows, lanes],
+                SLOT["ry"] + i, to_y(j),
+            ).start()
+        at = 0 if past == 1 else 1
+        send(
+            glow.at[low_rows(i, ring4(x, past)), cols_of(j)], rx.at[at, i, :, cols_of(j)],
+            SLOT["rx"] + i, to_x(past),
+        ).start()
+
+    order = (2, 3, 1, 0)
+    for j in order:
         term = jnp.dot(dkt[...], nbuf[:, cols_of(j)], preferred_element_type=F32)
         gup[ring4(y, j)] = term[:QK].astype(BF16)
         glow[:, cols_of(j)] = term[QK:].astype(BF16)
-        for i in range(CH):
-            rows = pl.ds(CK * i, CK)
-            if j == 2:
-                relay[i].append(Group(
-                    SLOT["qy"] + i, gup.at[0, rows],
-                    [(gup.at[ring4(y, 2), rows, pl.ds(at * PC, PC)], qy.at[at, rows], to_y(d))
-                     for at, d in enumerate((1, 3))],
-                ))
-                relay[i][0].start()
-            at = 0 if j in (2, 1) else 1
-            part_x = (
-                glow.at[low_rows(i, ring4(x, 2)), cols_of(j)], qx.at[i, j], to_x(1 + 2 * at)
-            )
-            send(part_x[0], part_x[1], SLOT["qx"] + i, part_x[2]).start()
-        for i in range(CH):
-            rows = pl.ds(CK * i, CK)
-            if j in (1, 3):
-                at = 0 if j == 1 else 1
-                lanes = pl.ds((1 - at) * PC, PC)
-                send(
-                    gup.at[ring4(y, j), rows, lanes], ry.at[at, rows, lanes],
-                    SLOT["ry"] + i, to_y(j),
-                ).start()
-            at = 1 if j in (2, 1) else 0
-            d = 1 + 2 * at
-            send(
-                glow.at[low_rows(i, ring4(x, d)), cols_of(j)], rx.at[at, i, :, cols_of(j)],
-                SLOT["rx"] + i, to_x(d),
-            ).start()
-    for i in range(CH):
-        rows = pl.ds(CK * i, CK)
+        issue(0, j)
+    for j in order:
+        issue(1, j)
+    def combine(i):
         relay[i].append(Group(SLOT["qx"] + i, qx.at[i], []))
-        stage1[i] += [
-            Group(SLOT["ry"] + i, gup.at[0, rows], []),
-            Group(SLOT["rx"] + i, rx.at[0, i], []),
-        ]
-
-    def combine(i):
         take(*relay[i])
         rows = slice(CK * i, CK * i + CK)
         late_y, late_x = [], []
@@ -423,11 +414,20 @@
                 )
         rows = pl.ds(CK * i, CK)
         stage1[i] += [
+            Group(SLOT["ry"] + i, gup.at[0, rows], []),
+            Group(SLOT["rx"] + i, rx.at[0, i], []),
             Group(SLOT["ry"] + CH + i, gup.at[0, rows], late_y),
             Group(SLOT["rx"] + CH + i, rx.at[0, i], late_x),
         ]
         go(*stage1[i][2:])
 
+    squares = jnp.sum(keys[...] * keys[...], axis=0, keepdims=True)
+    lown[...] = jnp.broadcast_to(jnp.sum(squares, axis=1, keepdims=True), (1, 128))
+    lsend = send(lown, lsib, SLOT["lsib"], sib)
+    lsend.start()
+    combine(0)
+    for j in order:
+        issue(2, j)
     take(lsend)
     lsh[mine] = lown[...] + lsib[...]
     lsends = Group(
@@ -510,19 +510,31 @@
     def gather(i):
         take(*agz[i])
         agx[i].append(Group(
-            SLOT["agx"] + i, fin.at[i, pl.ds(0, 3)],
-            [(fin.at[i, x], fin.at[i, x], to_x(d)) for d in (1, 3, 2)],
+            SLOT["agx"] + i, fin.at[i, pl.ds(0, 3 if i == CH - 1 else 2)],
+            [(fin.at[i, x], fin.at[i, x], to_x(d)) for d in ((1, 3, 2) if i == CH - 1 else (1, 3))],
         ))
         agx[i][0].start()
+
+    def forward(i):
+        take(agx[i][0])
+        behind = fin.at[i, ring4(x, 3), pl.ds(0, 2)]
+        ahead = fin.at[i, ring4(x, 1), pl.ds(2, 2)]
+        agx[i].append(Group(
+            SLOT["agf"] + i, fin.at[i, 0],
+            [(behind, behind, to_x(1)), (ahead, ahead, to_x(3))],
+        ))
+        agx[i][1].start()
 
     def drain(copies):
         for copy in copies:
             copy.wait_send()
 
     swaps = []
-    combine(0)
     combine(1)
+    reduce1(0)
     combine(2)
+    reduce1(1)
+    reduce2(0)
     drain([sib_w, sib_info, sib_tea, sib_hid, gsend, csend] + first + second)
     drain(handed.values())
 
@@ -532,10 +544,12 @@
             z_over(i).wait_send()
             z_in(i).wait_send()
 
-    reduce1(0)
-    reduce1(1)
     reduce1(2)
+    reduce2(1)
+    reduce3(0)
     drain([lsend] + sum(relay + stage1, []))
+    reduce2(2)
+    scatter(0)
     take(lsends)
     total = lsh[0]
     for i in range(1, 8):
@@ -546,18 +560,14 @@
         [(ldp.at[gid], ldp.at[gid], dev) for _, dev in dp_peers],
     )
     lsends2.start()
-    reduce2(0)
-    reduce2(1)
-    reduce3(0)
-    reduce2(2)
-    scatter(0)
     reduce3(1)
-    drain([lsends] + sum(stage2, []))
     scatter(1)
     gather(0)
     reduce3(2)
+    gather(1)
     scatter(2)
-    gather(1)
+    forward(0)
+    drain([lsends] + sum(stage2, []))
     take(lsends2)
     total = ldp[0]
     for i in range(1, 16):
@@ -565,9 +575,10 @@
     loss_o[...] = (total / (2.0 * KV * count))[:, 0:1]
     drain([lsends2] + sum(stage3, []) + swaps)
     gather(2)
+    forward(1)
     drain(agz[0] + agz[1] + agx[0])
     for i in range(CH):
-        take(*agx[i])
+        take(agx[i][-1])
     ordered = [
         fin[i, xx, 2 * side + l]
         for side in range(2) for i in range(CH) for xx in range(4) for l in range(2)
@@ -593,26 +604,26 @@
         copy.wait()
 
 
-def finish(key, gain, loss, loss_o, gain_o, key_o):
-    key_o[...] = key[...]
-
-    @pl.when(pl.program_id(0) == 0)
-    def _():
-        loss_o[...] = loss[...]
-        gain_o[...] = gain[...].reshape(SL)
+def finish(key, gain, loss, loss_o, gain_o, key_o, sem):
+    copy = pltpu.make_async_copy(key, key_o, sem)
+    copy.start()
+    loss_o[...] = loss[...]
+    gain_o[...] = gain[...].reshape(SL)
+    copy.wait()
 
 
 def body(hidden_in, teacher, norm_gain, w_key, group_rows, member):
     vm = pl.BlockSpec(memory_space=pltpu.VMEM)
     hbm = pl.BlockSpec(memory_space=pl.ANY)
+    far = pl.BlockSpec(memory_space=pltpu.HBM)
     loss, gain, key = pl.pallas_call(
         kernel,
         out_shape=(
             jax.ShapeDtypeStruct((1, 1), F32),
-            jax.ShapeDtypeStruct((1, SL), F32),
-            jax.ShapeDtypeStruct((SL, KV), F32),
+            pltpu.VMEM((1, SL), F32),
+            pltpu.VMEM((SL, KV), F32),
         ),
-        in_specs=[hbm, hbm, hbm, vm, vm, vm],
+        in_specs=[far, far, far, vm, vm, vm],
         out_specs=(vm, vm, hbm),
         scratch_shapes=[
             pltpu.VMEM((SL, KV), BF16),
@@ -657,7 +668,7 @@
             pltpu.SemaphoreType.DMA((3,)),
         ],
         compiler_params=pltpu.CompilerParams(
-            collective_id=0, has_side_effects=True, vmem_limit_bytes=62 * 2**20
+            collective_id=0, has_side_effects=True, vmem_limit_bytes=60 * 2**20
         ),
     )(hidden_in, teacher, w_key, norm_gain, group_rows, member)
     loss, grad_gain, grad_key = pl.pallas_call(
@@ -667,17 +678,10 @@
             jax.ShapeDtypeStruct((SL,), F32),
             jax.ShapeDtypeStruct((SL, KV), F32),
         ),
-        grid=(4,),
-        in_specs=[
-            pl.BlockSpec((SL // 4, KV), lambda i: (i, 0)),
-            pl.BlockSpec((1, SL), lambda i: (0, 0)),
-            pl.BlockSpec((1, 1), lambda i: (0, 0)),
-        ],
-        out_specs=(
-            pl.BlockSpec((1, 1), lambda i: (0, 0)),
-            pl.BlockSpec((SL,), lambda i: (0,)),
-            pl.BlockSpec((SL // 4, KV), lambda i: (i, 0)),
-        ),
+        in_specs=[hbm, vm, vm],
+        out_specs=(vm, vm, far),
+        scratch_shapes=[pltpu.SemaphoreType.DMA],
+        compiler_params=pltpu.CompilerParams(vmem_limit_bytes=8 * 2**20),
     )(key, gain, loss)
     return loss.reshape(()), grad_gain, grad_key
 

time: 96.2 us -> 89.7 us (0.932)
  Pallas kernels: 94.1 us -> 87.7 us
    pallas_call x1, Pallas kernels: 90 us -> 85.5 us  [body(): pl.pallas_call(kernel, out_shape=(jax.ShapeDtypeStruct((1, 1), F32), pltp...]
    pallas_call x1, Pallas kernels: 4.05 us -> 2.15 us  [body(): pl.pallas_call(finish, out_shape=(jax.ShapeDtypeStruct((1, 1), F32), jax....]
where the time goes in v6:
time: 89.7 us; the launch traced here: 89.6 us
  Pallas kernels  87.7 us (98%)
  between operations  1.93 us (2%)
    pallas_call x1, Pallas kernels, body(): pl.pallas_call(kernel, out_shape=(jax.ShapeDtypeStruct((1, 1), F32), pltp...  85.5 us
    pallas_call x1, Pallas kernels, body(): pl.pallas_call(finish, out_shape=(jax.ShapeDtypeStruct((1, 1), F32), jax....  2.15 us

profile of v6, /device:TPU:1, one launch (start us, length us, event | category | flops | bytes accessed | tf_op | source)
XLA Modules:
  0.0 89.6 jit_solution(15811130540860441054)
XLA Ops:
  1.9 85.5 %shard_map.85 = (f32[1,1]{1,0:T(1,128)}, f32[1,320]{1,0:T(1,128)S(1)}, f32[320,768]{1,0:T(8,128)S(1)}) custom-call(bf16[256,5120]{1,0:T(8,128)(2,1)} %hid.1, bf16[256,768]{1,0:T(8,128)(2,1)} %tea.1, bf16[320,768]{1,0:T(8,128)(2,1)} %w.1, bf16[320]{0:T(512)(128)(2,1)} %gain.1, s32[1]{0:T(128)S(6)} %copy.9.rows_of, s32[1,1]{1,0:T(1,128)S(6)} %copy.10.alive), custom_call_target="tpu_custom_call" | custom-call | tf_op jit(solution)/shard_map/pallas_call | solution.py:619
  87.4 2.2 %shard_map.86 = (f32[1,1]{1,0:T(1,128)}, f32[320]{0:T(512)}, f32[320,768]{1,0:T(8,128)}) custom-call(f32[320,768]{1,0:T(8,128)S(1)} %get-tuple-element.9.key, f32[1,320]{1,0:T(1,128)S(1)} %get-tuple-element.10.gain, f32[1,1]{1,0:T(1,128)} %get-tuple-element.11.loss), custom_call_target="tpu_custom_call" | custom-call | tf_op jit(solution)/shard_map/pallas_call | solution.py:674

commit v7 on v6

--- a/solution.py
+++ b/solution.py
@@ -51,7 +51,7 @@
 def kernel(
     hid, tea, w, gain, rows_of, alive, loss_o, gain_o, key_o,
     wv, hbuf, tbuf, wbuf, nbuf, inv, keys, dkt, gup, glow, qy, qx, ry, rx,
-    s2y, s2b, sx, sb, r2y, r2x, t3, t3b, r3, pown, prol, psib, fin, kt, info, isib, gfull, cbuf, lown, lsib, lsh, ldp,
+    s2y, s2b, sx, sb, r2y, r2x, t3, t3b, r3, pown, prol, psib, fin, last, kt, info, isib, gfull, cbuf, lown, lsib, lsh, ldp,
     lsem, ssem, rsem, zsem,
 ):
     zl, x = lax.axis_index("dp_0"), lax.axis_index("dp_1")
@@ -498,20 +498,25 @@
         swaps.append(send(prol.at[i], psib.at[i], SLOT["out"] + i, sib))
         swaps[i].start()
 
+    def done(i):
+        return last if i == CH - 1 else fin.at[i]
+
     def scatter(i):
         take(swaps[i])
-        fin[i, x, zl] = jnp.where(own, pown[i], psib[i])
+        to = done(i)
+        to[x, zl] = jnp.where(own, pown[i], psib[i]).astype(to.dtype)
         agz[i].append(Group(
-            SLOT["agz"] + i, fin.at[i, x, pl.ds(0, 3)],
-            [(fin.at[i, x, zl], fin.at[i, x, zl], {"dp_0": ring4(zl, d)}) for d in (1, 3, 2)],
+            SLOT["agz"] + i, to.at[x, pl.ds(0, 3)],
+            [(to.at[x, zl], to.at[x, zl], {"dp_0": ring4(zl, d)}) for d in (1, 3, 2)],
         ))
         agz[i][0].start()
 
     def gather(i):
         take(*agz[i])
+        to, steps = done(i), (1, 3, 2) if i == CH - 1 else (1, 3)
         agx[i].append(Group(
-            SLOT["agx"] + i, fin.at[i, pl.ds(0, 3 if i == CH - 1 else 2)],
-            [(fin.at[i, x], fin.at[i, x], to_x(d)) for d in ((1, 3, 2) if i == CH - 1 else (1, 3))],
+            SLOT["agx"] + i, to.at[pl.ds(0, len(steps))],
+            [(to.at[x], to.at[x], to_x(d)) for d in steps],
         ))
         agx[i][0].start()
 
@@ -580,7 +585,7 @@
     for i in range(CH):
         take(agx[i][-1])
     ordered = [
-        fin[i, xx, 2 * side + l]
+        done(i)[xx, 2 * side + l].astype(F32)
         for side in range(2) for i in range(CH) for xx in range(4) for l in range(2)
     ]
     kt[...] = jnp.transpose(jnp.concatenate(ordered, axis=0))
@@ -652,7 +657,8 @@
             pltpu.VMEM((CH, ZK, PC), F32),
             pltpu.VMEM((CH, ZK, PC), F32),
             pltpu.VMEM((CH, ZK, PC), F32),
-            pltpu.VMEM((CH, 4, 4, ZK, PC), F32),
+            pltpu.VMEM((CH - 1, 4, 4, ZK, PC), F32),
+            pltpu.VMEM((4, 4, ZK, PC), BF16),
             pltpu.VMEM((PC, HK), F32),
             pltpu.VMEM((1, PC + 128), F32),
             pltpu.VMEM((1, PC + 128), F32),

time: 89.7 us -> 88.6 us (0.988)
  Pallas kernels: 87.7 us -> 86.6 us
    pallas_call x1, Pallas kernels: 85.5 us -> 84.4 us  [body(): pl.pallas_call(kernel, out_shape=(jax.ShapeDtypeStruct((1, 1), F32), pltp...]
where the time goes in v7:
time: 88.6 us; the launch traced here: 88.5 us
  Pallas kernels  86.6 us (98%)
  between operations  1.93 us (2%)
    pallas_call x1, Pallas kernels, body(): pl.pallas_call(kernel, out_shape=(jax.ShapeDtypeStruct((1, 1), F32), pltp...  84.4 us
    pallas_call x1, Pallas kernels, body(): pl.pallas_call(finish, out_shape=(jax.ShapeDtypeStruct((1, 1), F32), jax....  2.15 us

profile of v7, /device:TPU:1, one launch (start us, length us, event | category | flops | bytes accessed | tf_op | source)
XLA Modules:
  0.0 88.5 jit_solution(4462980206283963097)
XLA Ops:
  1.9 84.4 %shard_map.85 = (f32[1,1]{1,0:T(1,128)}, f32[1,320]{1,0:T(1,128)S(1)}, f32[320,768]{1,0:T(8,128)S(1)}) custom-call(bf16[256,5120]{1,0:T(8,128)(2,1)} %hid.1, bf16[256,768]{1,0:T(8,128)(2,1)} %tea.1, bf16[320,768]{1,0:T(8,128)(2,1)} %w.1, bf16[320]{0:T(512)(128)(2,1)} %gain.1, s32[1]{0:T(128)S(6)} %copy.9.rows_of, s32[1,1]{1,0:T(1,128)S(6)} %copy.10.alive), custom_call_target="tpu_custom_call" | custom-call | tf_op jit(solution)/shard_map/pallas_call | solution.py:624
  86.3 2.2 %shard_map.86 = (f32[1,1]{1,0:T(1,128)}, f32[320]{0:T(512)}, f32[320,768]{1,0:T(8,128)}) custom-call(f32[320,768]{1,0:T(8,128)S(1)} %get-tuple-element.9.key, f32[1,320]{1,0:T(1,128)S(1)} %get-tuple-element.10.gain, f32[1,1]{1,0:T(1,128)} %get-tuple-element.11.loss), custom_call_target="tpu_custom_call" | custom-call | tf_op jit(solution)/shard_map/pallas_call | solution.py:680

commit v8 on v7

--- a/solution.py
+++ b/solution.py
@@ -43,13 +43,12 @@
 
 SLOT, N_SLOT = slots(
     *((name, 1) for name in ("info", "w", "tea", "hid", "lsib", "ginfo", "lsh", "cnt", "ldp")),
-    ("wy", 12), ("wx", 8), ("wz", 3), ("qy", CH), ("qx", CH), ("ry", 2 * CH), ("rx", 2 * CH),
-    ("s2y", CH), ("s2x", CH), ("s3", CH), ("agz", CH), ("agx", CH), ("agf", CH), ("out", CH),
+    ("wy", 12), ("wx", 8), ("wz", 3), ("via", CH), ("s1", CH), ("s2", CH), ("s3", CH), ("agz", CH), ("agx", CH), ("agf", CH), ("out", CH),
 )
 
 
 def kernel(
-    hid, tea, w, gain, rows_of, alive, loss_o, gain_o, key_o,
+    hid, tea, w, gain, rows_of, alive, loss_o, key_o,
     wv, hbuf, tbuf, wbuf, nbuf, inv, keys, dkt, gup, glow, qy, qx, ry, rx,
     s2y, s2b, sx, sb, r2y, r2x, t3, t3b, r3, pown, prol, psib, fin, last, kt, info, isib, gfull, cbuf, lown, lsib, lsh, ldp,
     lsem, ssem, rsem, zsem,
@@ -363,7 +362,7 @@
         rows = pl.ds(CK * i, CK)
         if j == 2:
             relay[i].append(Group(
-                SLOT["qy"] + i, gup.at[0, rows],
+                SLOT["via"] + i, gup.at[0, pl.ds(0, 2 * CK)],
                 [(gup.at[ring4(y, 2), rows, pl.ds(at * PC, PC)], qy.at[at, rows], to_y(d))
                  for at, d in enumerate((1, 3))],
             ))
@@ -371,19 +370,19 @@
         via, past = (1, 3) if j in (2, 1) else (3, 1)
         send(
             glow.at[low_rows(i, ring4(x, 2)), cols_of(j)], qx.at[i, j],
-            SLOT["qx"] + i, to_x(via),
+            SLOT["via"] + i, to_x(via),
         ).start()
         if j in (1, 3):
             at = 0 if j == 1 else 1
             lanes = pl.ds((1 - at) * PC, PC)
             send(
                 gup.at[ring4(y, j), rows, lanes], ry.at[at, rows, lanes],
-                SLOT["ry"] + i, to_y(j),
+                SLOT["s1"] + i, to_y(j),
             ).start()
         at = 0 if past == 1 else 1
         send(
             glow.at[low_rows(i, ring4(x, past)), cols_of(j)], rx.at[at, i, :, cols_of(j)],
-            SLOT["rx"] + i, to_x(past),
+            SLOT["s1"] + i, to_x(past),
         ).start()
 
     order = (2, 3, 1, 0)
@@ -395,7 +394,6 @@
     for j in order:
         issue(1, j)
     def combine(i):
-        relay[i].append(Group(SLOT["qx"] + i, qx.at[i], []))
         take(*relay[i])
         rows = slice(CK * i, CK * i + CK)
         late_y, late_x = [], []
@@ -412,14 +410,10 @@
                 late_x.append(
                     (glow.at[there, cols_of(j)], rx.at[at, i, :, cols_of(j)], to_x(d))
                 )
-        rows = pl.ds(CK * i, CK)
-        stage1[i] += [
-            Group(SLOT["ry"] + i, gup.at[0, rows], []),
-            Group(SLOT["rx"] + i, rx.at[0, i], []),
-            Group(SLOT["ry"] + CH + i, gup.at[0, rows], late_y),
-            Group(SLOT["rx"] + CH + i, rx.at[0, i], late_x),
-        ]
-        go(*stage1[i][2:])
+        stage1[i].append(Group(
+            SLOT["s1"] + i, gup.at[pl.ds(0, 2), pl.ds(0, 2 * CK)], late_y + late_x
+        ))
+        stage1[i][0].start()
 
     squares = jnp.sum(keys[...] * keys[...], axis=0, keepdims=True)
     lown[...] = jnp.broadcast_to(jnp.sum(squares, axis=1, keepdims=True), (1, 128))
@@ -450,7 +444,7 @@
         s2y[rows] = total
         s2b[rows] = total.astype(BF16)
         stage2[i].append(Group(
-            SLOT["s2y"] + i, r2y.at[i],
+            SLOT["s2"] + i, gup.at[0, pl.ds(0, 6 * XK)],
             [(s2b.at[low_rows(i, ring4(x, d))], r2y.at[i, d - 1], to_x(d)) for d in (1, 3, 2)],
         ))
         stage2[i][0].start()
@@ -462,10 +456,9 @@
             )
             if j:
                 sb[i, j - 1] = total.astype(BF16)
-                send(sb.at[i, j - 1], r2x.at[i, j - 1], SLOT["s2x"] + i, to_y(j)).start()
+                send(sb.at[i, j - 1], r2x.at[i, j - 1], SLOT["s2"] + i, to_y(j)).start()
             else:
                 sx[i] = total
-        stage2[i].append(Group(SLOT["s2x"] + i, r2x.at[i], []))
 
     def reduce2(i):
         take(*stage2[i])
@@ -596,40 +589,38 @@
         for half in range(2)
     ]
     go(*outs)
-    terms = (
-        kt[:SL, :] * wv[:, :HK].astype(F32) + kt[SL:, :] * wv[:, HK:].astype(F32)
-    )
-    summed = lax.dot_general(
-        jnp.ones((8, HK), F32), terms, (((1,), (1,)), ((), ())),
-        preferred_element_type=F32, precision=lax.Precision.HIGHEST,
-    )
-    gain_o[...] = summed[0:1, :] / own_gain
     drain(agz[2] + agx[1] + agx[2])
     for copy in outs:
         copy.wait()
 
 
-def finish(key, gain, loss, loss_o, gain_o, key_o, sem):
-    copy = pltpu.make_async_copy(key, key_o, sem)
-    copy.start()
+def finish(key, w, gain, loss, loss_o, gain_o, key_o, wv, sem):
+    read = pltpu.make_async_copy(w, wv, sem.at[0])
+    write = pltpu.make_async_copy(key, key_o, sem.at[1])
+    read.start()
+    write.start()
     loss_o[...] = loss[...]
-    gain_o[...] = gain[...].reshape(SL)
-    copy.wait()
+    read.wait()
+    summed = lax.dot_general(
+        jnp.ones((8, KV), F32), key[...] * wv[...].astype(F32), (((1,), (1,)), ((), ())),
+        preferred_element_type=F32, precision=lax.Precision.HIGHEST,
+    )
+    gain_o[...] = (summed[0:1, :] / gain[...].astype(F32).reshape(1, SL)).reshape(SL)
+    write.wait()
 
 
 def body(hidden_in, teacher, norm_gain, w_key, group_rows, member):
     vm = pl.BlockSpec(memory_space=pltpu.VMEM)
     hbm = pl.BlockSpec(memory_space=pl.ANY)
     far = pl.BlockSpec(memory_space=pltpu.HBM)
-    loss, gain, key = pl.pallas_call(
+    loss, key = pl.pallas_call(
         kernel,
         out_shape=(
             jax.ShapeDtypeStruct((1, 1), F32),
-            pltpu.VMEM((1, SL), F32),
             pltpu.VMEM((SL, KV), F32),
         ),
         in_specs=[far, far, far, vm, vm, vm],
-        out_specs=(vm, vm, hbm),
+        out_specs=(vm, hbm),
         scratch_shapes=[
             pltpu.VMEM((SL, KV), BF16),
             pltpu.VMEM((2, TOK, D), BF16),
@@ -684,11 +675,11 @@
             jax.ShapeDtypeStruct((SL,), F32),
             jax.ShapeDtypeStruct((SL, KV), F32),
         ),
-        in_specs=[hbm, vm, vm],
+        in_specs=[vm, far, vm, vm],
         out_specs=(vm, vm, far),
-        scratch_shapes=[pltpu.SemaphoreType.DMA],
+        scratch_shapes=[pltpu.VMEM((SL, KV), BF16), pltpu.SemaphoreType.DMA((2,))],
         compiler_params=pltpu.CompilerParams(vmem_limit_bytes=8 * 2**20),
-    )(key, gain, loss)
+    )(key, w_key, norm_gain, loss)
     return loss.reshape(()), grad_gain, grad_key
 
 

time: 88.6 us -> 88.1 us (level)
    pallas_call x1, Pallas kernels: 84.4 us -> 83.4 us  [body(): pl.pallas_call(kernel, out_shape=(jax.ShapeDtypeStruct((1, 1), F32), pltp...]
where the time goes in v8:
time: 88.1 us; the launch traced here: 87.9 us
  Pallas kernels  85.9 us (98%)
  between operations  2.02 us (2%)
    pallas_call x1, Pallas kernels, body(): pl.pallas_call(kernel, out_shape=(jax.ShapeDtypeStruct((1, 1), F32), pltp...  83.4 us
    pallas_call x1, Pallas kernels, body(): pl.pallas_call(finish, out_shape=(jax.ShapeDtypeStruct((1, 1), F32), jax....  2.45 us

profile of v8, /device:TPU:1, one launch (start us, length us, event | category | flops | bytes accessed | tf_op | source)
XLA Modules:
  0.0 87.9 jit_solution(12749607414296690172)
XLA Ops:
  0.6 0.0 copy-start
  0.6 0.0 copy-start.1
  2.0 83.4 %shard_map.85 = (f32[1,1]{1,0:T(1,128)}, f32[320,768]{1,0:T(8,128)S(1)}) custom-call(bf16[256,5120]{1,0:T(8,128)(2,1)} %hid.1, bf16[256,768]{1,0:T(8,128)(2,1)} %tea.1, bf16[320,768]{1,0:T(8,128)(2,1)} %w.3, bf16[320]{0:T(512)(128)(2,1)} %gain.3, s32[1]{0:T(128)S(6)} %copy.9.rows_of, s32[1,1]{1,0:T(1,128)S(6)} %copy.10.alive), custom_call_target="tpu_custom_call" | custom-call | tf_op jit(solution)/shard_map/pallas_call | solution.py:616
  85.5 0.0 copy-done
  85.5 0.0 copy-done.1
  85.5 2.4 %shard_map.86 = (f32[1,1]{1,0:T(1,128)}, f32[320]{0:T(512)}, f32[320,768]{1,0:T(8,128)}) custom-call(f32[320,768]{1,0:T(8,128)S(1)} %get-tuple-element.8.key, bf16[320,768]{1,0:T(8,128)(2,1)S(1)} %copy-done, bf16[320]{0:T(512)(128)(2,1)S(1)} %copy-done.1, f32[1,1]{1,0:T(1,128)} %get-tuple-element.9.loss), custom_call_target="tpu_custom_call" | custom-call | tf_op jit(solution)/shard_map/pallas_call | solution.py:671
Async XLA Ops:
  0.6 84.8 %copy-start = (bf16[320,768]{1,0:T(8,128)(2,1)S(1)}, bf16[320,768]{1,0:T(8,128)(2,1)}, u32[]{:S(2)}) copy-start(bf16[320,768]{1,0:T(8,128)(2,1)} %w.3) | copy-start | bytes 1474564
  0.6 84.8 %copy-start.1 = (bf16[320]{0:T(512)(128)(2,1)S(1)}, bf16[320]{0:T(512)(128)(2,1)}, u32[]{:S(2)}) copy-start(bf16[320]{0:T(512)(128)(2,1)} %gain.3) | copy-start | bytes 1924
